TPU v7x, 128 devices: a whole 4x4x4 slice. The times are simulated.
128 devices in a mesh: gx: 8 (over z_lo, y), gy: 16 (over z_hi, x, core).
Axes of the slice: x: 4, y: 4, z: 4 (z_hi: 2, z_lo: 2; z = z_hi * 2 + z_lo), core: 2. Of those that a mesh axis runs over, the one named last changes fastest.
Arguments:
- u_wind: float32 [60, 512, 2048], P(None, 'gx', 'gy'), may hold values from -6 to 6
- v_wind: float32 [60, 512, 2048], P(None, 'gx', 'gy'), may hold values from -6 to 6
- w_wind: float32 [60, 512, 2048], P(None, 'gx', 'gy'), may hold values from -3 to 3
- pressure: float32 [60, 512, 2048], P(None, 'gx', 'gy'), may hold values from -6 to 6
- vert_coef: float32 [512, 2048], P('gx', 'gy'), may hold values from 0.2 to 5
- we_slab: float32 [2, 3, 60, 5, 2048], P(None, None, None, None, ('gy', 'gx')), may hold values from -8 to 8
- sn_slab: float32 [2, 3, 60, 5, 512], P(None, None, None, None, ('gx', 'gy')), may hold values from -8 to 8
- relax_width: int32 [512, 2048], P('gx', 'gy'), may hold values from 2 to 5
Outputs:
- u_out: float32 [60, 512, 2048], P(None, 'gx', 'gy')
- v_out: float32 [60, 512, 2048], P(None, 'gx', 'gy')
- w_out: float32 [60, 512, 2048], P(None, 'gx', 'gy')
- p_out: float32 [60, 512, 2048], P(None, 'gx', 'gy')
All inputs are finite; a program needn't handle non-finite values.
Results may differ from a plain program's by a relative error of at most 0.0001.
Values sent between devices are 32-bit elements; how exact they have to be, the bound alone decides.
A program may use at most 192 MiB of HBM per device.

v0:
```python
import jax
import jax.numpy as jnp
from jax import lax
from jax.sharding import PartitionSpec as P

SUBSTEPS = 6


accel = 0.3
spread = 0.3
buoyancy = 0.5


def in_order(pieces, dim):
    pieces = jnp.moveaxis(pieces, 0, dim)
    dims = pieces.shape
    return pieces.reshape(*dims[:dim], dims[dim] * dims[dim + 1], *dims[dim + 2 :])


def sent_to_all(value, axis):
    size = lax.axis_size(axis)
    return lax.all_to_all(
        jnp.broadcast_to(value[None], (size, *value.shape)), axis, 0, 0, tiled=True
    )


def gather_directly(value, axis, dim):
    return in_order(sent_to_all(value, axis), dim)


def passed_along(block, axis, distance):
    devices = range(lax.axis_size(axis))
    route = [(i - distance, i) for i in devices if i - distance in devices]
    return lax.ppermute(block, axis, route)


def factorize(coef, levels):
    cees = []
    denoms = []
    prev_c = jnp.zeros_like(coef)
    for level in range(levels):
        denom = 1.0 + 2.0 * coef + coef * prev_c
        next_c = -coef / denom
        cees.append(next_c)
        denoms.append(denom)
        prev_c = next_c
    return (cees, denoms)


def tri_solve(coef, factors, rhs):
    cees, denoms = factors
    levels = rhs.shape[0]
    dees = []
    prev_d = jnp.zeros_like(coef)
    for level in range(levels):
        next_d = (rhs[level] + coef * prev_d) / denoms[level]
        dees.append(next_d)
        prev_d = next_d
    solved = [None] * levels
    above = jnp.zeros_like(coef)
    for level in range(levels - 1, -1, -1):
        above = dees[level] - cees[level] * above
        solved[level] = above
    return jnp.stack(solved, axis=0)


def blend(field, rows_k, cols_k, xpos, ypos, nx_total, ny_total, rate):
    band = rows_k.shape[2]
    size_x = field.shape[1]
    size_y = field.shape[2]
    west = jnp.pad(rows_k[0], ((0, 0), (0, size_x - band), (0, 0)))
    east = jnp.pad(rows_k[1][:, ::-1, :], ((0, 0), (size_x - band, 0), (0, 0)))
    south = jnp.pad(jnp.transpose(cols_k[0], (0, 2, 1)), ((0, 0), (0, 0), (0, size_y - band)))
    north = jnp.pad(
        jnp.transpose(cols_k[1][:, ::-1, :], (0, 2, 1)), ((0, 0), (0, 0), (size_y - band, 0))
    )
    weight_w = jnp.maximum(rate - xpos[:, None], 0.0) / rate
    weight_e = jnp.maximum(rate - (nx_total - 1.0 - xpos)[:, None], 0.0) / rate
    weight_s = jnp.maximum(rate - ypos[None, :], 0.0) / rate
    weight_n = jnp.maximum(rate - (ny_total - 1.0 - ypos)[None, :], 0.0) / rate
    field = field + weight_w[None] * (west - field)
    field = field + weight_e[None] * (east - field)
    field = field + weight_s[None] * (south - field)
    field = field + weight_n[None] * (north - field)
    return field


def column_part(u_new, v_new, west_u, south_v, w_old, p_old, coef, factors):
    diverge = u_new - west_u + (v_new - south_v)
    sectioned = p_old - spread * diverge
    above_q = jnp.concatenate([sectioned[1:], jnp.zeros_like(sectioned[:1])], axis=0)
    rhs = w_old + buoyancy * (sectioned - above_q)
    w_new = tri_solve(coef, factors, rhs)
    below_w = jnp.concatenate([jnp.zeros_like(w_new[:1]), w_new[:-1]], axis=0)
    p_new = sectioned - buoyancy * (w_new - below_w)
    return (w_new, p_new)


def per_device(u_wind, v_wind, w_wind, pressure, vert_coef, we_slab, sn_slab, relax_width):
    edge_vals = gather_directly(we_slab, "gx", 4)
    side_vals = lax.all_gather(sn_slab, "gy", axis=4, tiled=True)
    size_x = pressure.shape[1]
    size_y = pressure.shape[2]
    levels = pressure.shape[0]
    col_index = lax.axis_index("gx")
    row_index = lax.axis_index("gy")
    xpos = (col_index * size_x + jnp.arange(size_x, dtype=jnp.int32)).astype(jnp.float32)
    ypos = (row_index * size_y + jnp.arange(size_y, dtype=jnp.int32)).astype(jnp.float32)
    nx_total = float(size_x * lax.axis_size("gx"))
    ny_total = float(size_y * lax.axis_size("gy"))
    rate = relax_width.astype(jnp.float32)
    fields = []
    for index, field in enumerate((u_wind, v_wind, pressure)):
        fields.append(
            blend(
                field,
                edge_vals[:, index],
                side_vals[:, index],
                xpos,
                ypos,
                nx_total,
                ny_total,
                rate,
            )
        )
    u_now, v_now, p_now = fields
    w_now = w_wind
    factors = factorize(vert_coef, levels)
    for step in range(SUBSTEPS):
        east_rim = passed_along(p_now[:, :1, :], "gx", -1)
        north_rim = passed_along(p_now[:, :, :1], "gy", -1)
        east_p = jnp.concatenate([p_now[:, 1:, :], east_rim], axis=1)
        north_p = jnp.concatenate([p_now[:, :, 1:], north_rim], axis=2)
        u_now = u_now - accel * (east_p - p_now)
        v_now = v_now - accel * (north_p - p_now)
        west_rim = passed_along(u_now[:, -1:, :], "gx", 1)
        south_rim = passed_along(v_now[:, :, -1:], "gy", 1)
        west_u = jnp.concatenate([west_rim, u_now[:, :-1, :]], axis=1)
        south_v = jnp.concatenate([south_rim, v_now[:, :, :-1]], axis=2)
        w_now, p_now = column_part(u_now, v_now, west_u, south_v, w_now, p_now, vert_coef, factors)
    return (u_now, v_now, w_now, p_now)


def solution(mesh):
    placed = (
        P(None, "gx", "gy"),
        P(None, "gx", "gy"),
        P(None, "gx", "gy"),
        P(None, "gx", "gy"),
        P("gx", "gy"),
        P(None, None, None, None, ("gy", "gx")),
        P(None, None, None, None, ("gx", "gy")),
        P("gx", "gy"),
    )
    return jax.shard_map(
        per_device,
        mesh=mesh,
        in_specs=placed,
        out_specs=(
            P(None, "gx", "gy"),
            P(None, "gx", "gy"),
            P(None, "gx", "gy"),
            P(None, "gx", "gy"),
        ),
        check_vma=False,
    )
```

profile of v0, /device:TPU:88, one launch (start us, length us, event | category | flops | bytes accessed | tf_op | source)
XLA Modules:
  0.0 398.4 jit_solution(15434892561254640329)
XLA Ops:
  5.9 5.7 %all-to-all-start = ((f32[8,1,28800]{2,1,0:T(1,128)}), f32[8,1,28800]{2,1,0:T(1,128)S(1)}, u32[]{:S(2)}, u32[]{:S(2)}) async-start(f32[8,1,28800]{2,1,0:T(1,128)} %reshape.57), calls=%async_computation | async-start | bytes 1843200 | tf_op jit(solution)/shard_map/all_to_all | solution.py:22
  11.6 24.6 %all_gather.3 = f32[2,3,60,5,64]{2,0,3,1,4:T(2,128)S(1)} all-gather(f32[2,3,60,5,4]{2,0,3,1,4:T(2,128)S(1)} %copy.2894), channel_id=1, replica_groups=mesh['gx'=8,'gy'=16] {'gy'}, dimensions={4}, use_global_device_ids=true | all-gather | bytes 489600 | tf_op jit(solution)/shard_map/all_gather | solution.py:101
  94.7 7.6 %fusion.6 = (f32[60,64,128]{2,1,0:T(8,128)S(1)}, f32[60,64,128]{2,1,0:T(8,128)S(1)}) fusion(f32[60,64,128]{2,1,0:T(8,128)S(1)} %multiply_add_fusion.6, f32[60,64,1]{2,1,0:T(8,128)} %copy.2906, f32[60,64,127]{2,1,0:T(8,128)} %slice.1762, f32[60,64,5]{2,1,0:T(8,128)} %bitcast.4718, f32[60,64,5]{2,1,0:T(8,128)} %bitcast.4717, f32[60,5,128]{2,1,0:T(8,128)S(1)} %rev.22, ...), kind=kLoop, calls=%fused_computation.9 | loop fusion | flops 15728640 | bytes 14815232 | tf_op jit(solution)/shard_map/sub | solution.py:135
  103.5 5.4 %collective-permute-start.1 = (f32[60,1,128]{2,1,0:T(1,128)S(1)}, f32[60,1,128]{2,1,0:T(1,128)S(1)}, u32[]{:S(2)}, u32[]{:S(2)}) collective-permute-start(f32[60,1,128]{2,1,0:T(1,128)S(1)} %slice.1756), channel_id=1, source_target_pairs={{0,16},{16,32},{32,48},{48,64},{64,80},{80,96},{96,112},{1,17},{17... | collective-permute-start | bytes 92168 | tf_op jit(solution)/shard_map/ppermute | solution.py:34
  115.5 6.3 %collective-permute-done.3 = f32[60,64,1]{1,2,0:T(1,128)S(1)} collective-permute-done((f32[60,64,1]{1,2,0:T(1,128)S(1)}, f32[60,64,1]{1,2,0:T(1,128)S(1)}, u32[]{:S(2)}, u32[]{:S(2)}) %collective-permute-start.3) | collective-permute-done | bytes 15392 | tf_op jit(solution)/shard_map/ppermute | solution.py:34
  147.4 5.1 %fusion.13 = (f32[60,64,128]{2,1,0:T(8,128)S(1)}, f32[60,64,128]{2,1,0:T(8,128)S(1)}) fusion(f32[60,64,128]{2,1,0:T(8,128)} %copy-done.2, f32[60,64,128]{2,1,0:T(8,128)S(1)} %multiply_subtract_fusion.5, f32[60,64,1]{2,1,0:T(8,128)} %copy.2910, f32[60,64,127]{2,1,0:T(8,128)} %slice.1831, f32[60,64,128]{2,1,0:T(8,128)} %copy-done.7, ...), kind=kLoop, calls=%fused_computation.20 | loop fusion | flops 3932160 | bytes 13762560 | tf_op jit(solution)/shard_map/sub | solution.py:135
  154.5 6.0 %collective-permute-start.5 = (f32[60,1,128]{2,1,0:T(1,128)}, f32[60,1,128]{2,1,0:T(1,128)}, u32[]{:S(2)}, u32[]{:S(2)}) collective-permute-start(f32[60,1,128]{2,1,0:T(1,128)} %slice.1829), channel_id=1, source_target_pairs={{0,16},{16,32},{32,48},{48,64},{64,80},{80,96},{96,112},{1,17},{17... | collective-permute-start | bytes 92168 | tf_op jit(solution)/shard_map/ppermute | solution.py:34
  167.4 6.8 %collective-permute-done.7 = f32[60,64,1]{1,2,0:T(1,128)} collective-permute-done((f32[60,64,1]{1,2,0:T(1,128)}, f32[60,64,1]{1,2,0:T(1,128)}, u32[]{:S(2)}, u32[]{:S(2)}) %collective-permute-start.7) | collective-permute-done | bytes 15392 | tf_op jit(solution)/shard_map/ppermute | solution.py:34
  176.9 5.0 %fusion.11 = f32[60,64,128]{2,1,0:T(8,128)S(1)} fusion(f32[60,64,128]{2,1,0:T(8,128)S(1)} %multiply_subtract_fusion.5, f32[60,64,128]{2,1,0:T(8,128)} %copy-done.8, f32[60,63,128]{2,1,0:T(8,128)} %bitcast.4709, f32[60,1,128]{2,1,0:T(1,128)} %collective-permute-done.5, f32[60,64,128]{2,1,0:T(8,128)} %copy-done.3, f32[60,64,127]{2,1,0:T(8,128)} %bitcast.4704, ...), kind=kLoop, calls=%fused_computation.17 | loop fusion | flops 3440640 | bytes 11796480 | tf_op jit(solution)/shard_map/sub | solution.py:90
  199.8 5.1 %fusion.20 = (f32[60,64,128]{2,1,0:T(8,128)S(1)}, f32[60,64,128]{2,1,0:T(8,128)S(1)}) fusion(f32[60,64,128]{2,1,0:T(8,128)} %copy-done.3, f32[60,64,128]{2,1,0:T(8,128)S(1)} %multiply_subtract_fusion.4, f32[60,64,1]{2,1,0:T(8,128)} %copy.2914, f32[60,64,127]{2,1,0:T(8,128)} %slice.1900, f32[60,64,128]{2,1,0:T(8,128)} %copy-done.8, ...), kind=kLoop, calls=%fused_computation.31 | loop fusion | flops 3932160 | bytes 13762560 | tf_op jit(solution)/shard_map/sub | solution.py:135
  206.8 6.0 %collective-permute-start.9 = (f32[60,1,128]{2,1,0:T(1,128)}, f32[60,1,128]{2,1,0:T(1,128)}, u32[]{:S(2)}, u32[]{:S(2)}) collective-permute-start(f32[60,1,128]{2,1,0:T(1,128)} %slice.1898), channel_id=1, source_target_pairs={{0,16},{16,32},{32,48},{48,64},{64,80},{80,96},{96,112},{1,17},{17... | collective-permute-start | bytes 92168 | tf_op jit(solution)/shard_map/ppermute | solution.py:34
  219.8 6.8 %collective-permute-done.11 = f32[60,64,1]{1,2,0:T(1,128)} collective-permute-done((f32[60,64,1]{1,2,0:T(1,128)}, f32[60,64,1]{1,2,0:T(1,128)}, u32[]{:S(2)}, u32[]{:S(2)}) %collective-permute-start.11) | collective-permute-done | bytes 15392 | tf_op jit(solution)/shard_map/ppermute | solution.py:34
  229.3 5.0 %fusion.18 = f32[60,64,128]{2,1,0:T(8,128)S(1)} fusion(f32[60,64,128]{2,1,0:T(8,128)S(1)} %multiply_subtract_fusion.4, f32[60,64,128]{2,1,0:T(8,128)} %copy-done.9, f32[60,63,128]{2,1,0:T(8,128)} %bitcast.4710, f32[60,1,128]{2,1,0:T(1,128)} %collective-permute-done.9, f32[60,64,128]{2,1,0:T(8,128)} %copy-done.4, f32[60,64,127]{2,1,0:T(8,128)} %bitcast.4705, ...), kind=kLoop, calls=%fused_computation.28 | loop fusion | flops 3440640 | bytes 11796480 | tf_op jit(solution)/shard_map/sub | solution.py:90
  252.1 5.1 %fusion.27 = (f32[60,64,128]{2,1,0:T(8,128)S(1)}, f32[60,64,128]{2,1,0:T(8,128)S(1)}) fusion(f32[60,64,128]{2,1,0:T(8,128)} %copy-done.4, f32[60,64,128]{2,1,0:T(8,128)S(1)} %multiply_subtract_fusion.3, f32[60,64,1]{2,1,0:T(8,128)} %copy.2918, f32[60,64,127]{2,1,0:T(8,128)} %slice.1969, f32[60,64,128]{2,1,0:T(8,128)} %copy-done.9, ...), kind=kLoop, calls=%fused_computation.42 | loop fusion | flops 3932160 | bytes 13762560 | tf_op jit(solution)/shard_map/sub | solution.py:135
  259.2 6.0 %collective-permute-start.13 = (f32[60,1,128]{2,1,0:T(1,128)}, f32[60,1,128]{2,1,0:T(1,128)}, u32[]{:S(2)}, u32[]{:S(2)}) collective-permute-start(f32[60,1,128]{2,1,0:T(1,128)} %slice.1967), channel_id=1, source_target_pairs={{0,16},{16,32},{32,48},{48,64},{64,80},{80,96},{96,112},{1,17},{17... | collective-permute-start | bytes 92168 | tf_op jit(solution)/shard_map/ppermute | solution.py:34
  272.2 6.8 %collective-permute-done.15 = f32[60,64,1]{1,2,0:T(1,128)} collective-permute-done((f32[60,64,1]{1,2,0:T(1,128)}, f32[60,64,1]{1,2,0:T(1,128)}, u32[]{:S(2)}, u32[]{:S(2)}) %collective-permute-start.15) | collective-permute-done | bytes 15392 | tf_op jit(solution)/shard_map/ppermute | solution.py:34
  304.5 5.1 %fusion.34 = (f32[60,64,128]{2,1,0:T(8,128)S(1)}, f32[60,64,128]{2,1,0:T(8,128)S(1)}) fusion(f32[60,64,128]{2,1,0:T(8,128)} %copy-done.5, f32[60,64,128]{2,1,0:T(8,128)S(1)} %multiply_subtract_fusion.2, f32[60,64,1]{2,1,0:T(8,128)} %copy.2922, f32[60,64,127]{2,1,0:T(8,128)} %slice.2038, f32[60,64,128]{2,1,0:T(8,128)} %copy-done.10, ...), kind=kLoop, calls=%fused_computation.53 | loop fusion | flops 3932160 | bytes 13762560 | tf_op jit(solution)/shard_map/sub | solution.py:135
  311.5 6.0 %collective-permute-start.17 = (f32[60,1,128]{2,1,0:T(1,128)}, f32[60,1,128]{2,1,0:T(1,128)}, u32[]{:S(2)}, u32[]{:S(2)}) collective-permute-start(f32[60,1,128]{2,1,0:T(1,128)} %slice.2036), channel_id=1, source_target_pairs={{0,16},{16,32},{32,48},{48,64},{64,80},{80,96},{96,112},{1,17},{17... | collective-permute-start | bytes 92168 | tf_op jit(solution)/shard_map/ppermute | solution.py:34
  324.8 6.5 %collective-permute-done.19 = f32[60,64,1]{1,2,0:T(1,128)} collective-permute-done((f32[60,64,1]{1,2,0:T(1,128)}, f32[60,64,1]{1,2,0:T(1,128)}, u32[]{:S(2)}, u32[]{:S(2)}) %collective-permute-start.19) | collective-permute-done | bytes 15392 | tf_op jit(solution)/shard_map/ppermute | solution.py:34
  334.0 5.0 %fusion.32 = f32[60,64,128]{2,1,0:T(8,128)S(1)} fusion(f32[60,64,128]{2,1,0:T(8,128)S(1)} %multiply_subtract_fusion.2, f32[60,64,128]{2,1,0:T(8,128)} %copy-done.11, f32[60,63,128]{2,1,0:T(8,128)} %bitcast.4712, f32[60,1,128]{2,1,0:T(1,128)} %collective-permute-done.17, f32[60,64,128]{2,1,0:T(8,128)} %copy-done.6, f32[60,64,127]{2,1,0:T(8,128)} %bitcast.4707, ...), kind=kLoop, calls=%fused_computation.50 | loop fusion | flops 3440640 | bytes 11796480 | tf_op jit(solution)/shard_map/sub | solution.py:90
  356.9 5.1 %fusion.38 = (f32[60,64,128]{2,1,0:T(8,128)S(1)}, f32[60,64,128]{2,1,0:T(8,128)S(1)}) fusion(f32[60,64,128]{2,1,0:T(8,128)} %copy-done.6, f32[60,64,128]{2,1,0:T(8,128)S(1)} %multiply_subtract_fusion.1, f32[60,64,1]{2,1,0:T(8,128)} %copy.2926, f32[60,64,127]{2,1,0:T(8,128)} %slice.2105, f32[60,64,128]{2,1,0:T(8,128)} %copy-done.11, ...), kind=kLoop, calls=%fused_computation.60 | loop fusion | flops 3932160 | bytes 13762560 | tf_op jit(solution)/shard_map/sub | solution.py:135
  364.0 6.0 %collective-permute-start.22 = (f32[60,1,128]{2,1,0:T(1,128)}, f32[60,1,128]{2,1,0:T(1,128)}, u32[]{:S(2)}, u32[]{:S(2)}) collective-permute-start(f32[60,1,128]{2,1,0:T(1,128)} %slice.2107), channel_id=1, source_target_pairs={{0,16},{16,32},{32,48},{48,64},{64,80},{80,96},{96,112},{1,17},{17... | collective-permute-start | bytes 92168 | tf_op jit(solution)/shard_map/ppermute | solution.py:34
  377.0 6.8 %collective-permute-done.23 = f32[60,64,1]{1,2,0:T(1,128)} collective-permute-done((f32[60,64,1]{1,2,0:T(1,128)}, f32[60,64,1]{1,2,0:T(1,128)}, u32[]{:S(2)}, u32[]{:S(2)}) %collective-permute-start.23) | collective-permute-done | bytes 15392 | tf_op jit(solution)/shard_map/ppermute | solution.py:34
  386.5 5.1 %fusion.41 = f32[60,64,128]{2,1,0:T(8,128)S(1)} fusion(f32[60,64,128]{2,1,0:T(8,128)S(1)} %multiply_subtract_fusion.1, f32[60,64,128]{2,1,0:T(8,128)} %copy-done.14, f32[60,63,128]{2,1,0:T(8,128)} %bitcast.4714, f32[60,1,128]{2,1,0:T(1,128)} %collective-permute-done.22, f32[60,64,128]{2,1,0:T(8,128)} %copy-done.12, f32[60,64,127]{2,1,0:T(8,128)} %bitcast.4713, ...), kind=kLoop, calls=%fused_computation.64 | loop fusion | flops 3440640 | bytes 11796480 | tf_op jit(solution)/shard_map/sub | solution.py:90
  (681 shorter events, 234.3 us)
Async XLA Ops:
  5.9 39.7 %all-to-all-start = ((f32[8,1,28800]{2,1,0:T(1,128)}), f32[8,1,28800]{2,1,0:T(1,128)S(1)}, u32[]{:S(2)}, u32[]{:S(2)}) async-start(f32[8,1,28800]{2,1,0:T(1,128)} %reshape.57), calls=%async_computation | async-start | bytes 1843200 | tf_op jit(solution)/shard_map/all_to_all | solution.py:22
  60.4 34.2 %collective-permute-start = (f32[60,1,128]{2,1,0:T(1,128)}, f32[60,1,128]{2,1,0:T(1,128)}, u32[]{:S(2)}, u32[]{:S(2)}) collective-permute-start(f32[60,1,128]{2,1,0:T(1,128)} %slice.1755), channel_id=1, source_target_pairs={{16,0},{32,16},{48,32},{64,48},{80,64},{96,80},{112,96},{17,1},{33... | collective-permute-start | bytes 92168 | tf_op jit(solution)/shard_map/ppermute | solution.py:34
  65.0 27.0 %collective-permute-start.2 = (f32[60,64,1]{1,2,0:T(1,128)}, f32[60,64,1]{1,2,0:T(1,128)}, u32[]{:S(2)}, u32[]{:S(2)}) collective-permute-start(f32[60,64,1]{1,2,0:T(1,128)} %copy.2905), channel_id=1, source_target_pairs={{1,0},{2,1},{3,2},{4,3},{5,4},{6,5},{7,6},{8,7},{9,8},{10,9},{11,1... | collective-permute-start | bytes 46088 | tf_op jit(solution)/shard_map/ppermute | solution.py:34
  103.5 20.2 %collective-permute-start.1 = (f32[60,1,128]{2,1,0:T(1,128)S(1)}, f32[60,1,128]{2,1,0:T(1,128)S(1)}, u32[]{:S(2)}, u32[]{:S(2)}) collective-permute-start(f32[60,1,128]{2,1,0:T(1,128)S(1)} %slice.1756), channel_id=1, source_target_pairs={{0,16},{16,32},{32,48},{48,64},{64,80},{80,96},{96,112},{1,17},{17... | collective-permute-start | bytes 92168 | tf_op jit(solution)/shard_map/ppermute | solution.py:34
  113.0 8.8 %collective-permute-start.3 = (f32[60,64,1]{1,2,0:T(1,128)S(1)}, f32[60,64,1]{1,2,0:T(1,128)S(1)}, u32[]{:S(2)}, u32[]{:S(2)}) collective-permute-start(f32[60,64,1]{1,2,0:T(1,128)S(1)} %copy.2907), channel_id=1, source_target_pairs={{0,1},{1,2},{2,3},{3,4},{4,5},{5,6},{6,7},{7,8},{8,9},{9,10},{10,1... | collective-permute-start | bytes 46088 | tf_op jit(solution)/shard_map/ppermute | solution.py:34
  136.3 11.1 %collective-permute-start.4 = (f32[60,1,128]{2,1,0:T(1,128)}, f32[60,1,128]{2,1,0:T(1,128)}, u32[]{:S(2)}, u32[]{:S(2)}) collective-permute-start(f32[60,1,128]{2,1,0:T(1,128)} %slice.1828), channel_id=1, source_target_pairs={{16,0},{32,16},{48,32},{64,48},{80,64},{96,80},{112,96},{17,1},{33... | collective-permute-start | bytes 92168 | tf_op jit(solution)/shard_map/ppermute | solution.py:34
  139.4 5.3 %collective-permute-start.6 = (f32[60,64,1]{1,2,0:T(1,128)}, f32[60,64,1]{1,2,0:T(1,128)}, u32[]{:S(2)}, u32[]{:S(2)}) collective-permute-start(f32[60,64,1]{1,2,0:T(1,128)} %copy.2909), channel_id=1, source_target_pairs={{1,0},{2,1},{3,2},{4,3},{5,4},{6,5},{7,6},{8,7},{9,8},{10,9},{11,1... | collective-permute-start | bytes 46088 | tf_op jit(solution)/shard_map/ppermute | solution.py:34
  154.5 22.5 %collective-permute-start.5 = (f32[60,1,128]{2,1,0:T(1,128)}, f32[60,1,128]{2,1,0:T(1,128)}, u32[]{:S(2)}, u32[]{:S(2)}) collective-permute-start(f32[60,1,128]{2,1,0:T(1,128)} %slice.1829), channel_id=1, source_target_pairs={{0,16},{16,32},{32,48},{48,64},{64,80},{80,96},{96,112},{1,17},{17... | collective-permute-start | bytes 92168 | tf_op jit(solution)/shard_map/ppermute | solution.py:34
  165.1 9.1 %collective-permute-start.7 = (f32[60,64,1]{1,2,0:T(1,128)}, f32[60,64,1]{1,2,0:T(1,128)}, u32[]{:S(2)}, u32[]{:S(2)}) collective-permute-start(f32[60,64,1]{1,2,0:T(1,128)} %copy.2911), channel_id=1, source_target_pairs={{0,1},{1,2},{2,3},{3,4},{4,5},{5,6},{6,7},{7,8},{8,9},{9,10},{10,1... | collective-permute-start | bytes 46088 | tf_op jit(solution)/shard_map/ppermute | solution.py:34
  188.6 11.1 %collective-permute-start.8 = (f32[60,1,128]{2,1,0:T(1,128)}, f32[60,1,128]{2,1,0:T(1,128)}, u32[]{:S(2)}, u32[]{:S(2)}) collective-permute-start(f32[60,1,128]{2,1,0:T(1,128)} %slice.1897), channel_id=1, source_target_pairs={{16,0},{32,16},{48,32},{64,48},{80,64},{96,80},{112,96},{17,1},{33... | collective-permute-start | bytes 92168 | tf_op jit(solution)/shard_map/ppermute | solution.py:34
  191.8 5.3 %collective-permute-start.10 = (f32[60,64,1]{1,2,0:T(1,128)}, f32[60,64,1]{1,2,0:T(1,128)}, u32[]{:S(2)}, u32[]{:S(2)}) collective-permute-start(f32[60,64,1]{1,2,0:T(1,128)} %copy.2913), channel_id=1, source_target_pairs={{1,0},{2,1},{3,2},{4,3},{5,4},{6,5},{7,6},{8,7},{9,8},{10,9},{11,1... | collective-permute-start | bytes 46088 | tf_op jit(solution)/shard_map/ppermute | solution.py:34
  206.8 22.5 %collective-permute-start.9 = (f32[60,1,128]{2,1,0:T(1,128)}, f32[60,1,128]{2,1,0:T(1,128)}, u32[]{:S(2)}, u32[]{:S(2)}) collective-permute-start(f32[60,1,128]{2,1,0:T(1,128)} %slice.1898), channel_id=1, source_target_pairs={{0,16},{16,32},{32,48},{48,64},{64,80},{80,96},{96,112},{1,17},{17... | collective-permute-start | bytes 92168 | tf_op jit(solution)/shard_map/ppermute | solution.py:34
  217.5 9.1 %collective-permute-start.11 = (f32[60,64,1]{1,2,0:T(1,128)}, f32[60,64,1]{1,2,0:T(1,128)}, u32[]{:S(2)}, u32[]{:S(2)}) collective-permute-start(f32[60,64,1]{1,2,0:T(1,128)} %copy.2915), channel_id=1, source_target_pairs={{0,1},{1,2},{2,3},{3,4},{4,5},{5,6},{6,7},{7,8},{8,9},{9,10},{10,1... | collective-permute-start | bytes 46088 | tf_op jit(solution)/shard_map/ppermute | solution.py:34
  241.0 11.1 %collective-permute-start.12 = (f32[60,1,128]{2,1,0:T(1,128)}, f32[60,1,128]{2,1,0:T(1,128)}, u32[]{:S(2)}, u32[]{:S(2)}) collective-permute-start(f32[60,1,128]{2,1,0:T(1,128)} %slice.1966), channel_id=1, source_target_pairs={{16,0},{32,16},{48,32},{64,48},{80,64},{96,80},{112,96},{17,1},{33... | collective-permute-start | bytes 92168 | tf_op jit(solution)/shard_map/ppermute | solution.py:34
  244.2 5.3 %collective-permute-start.14 = (f32[60,64,1]{1,2,0:T(1,128)}, f32[60,64,1]{1,2,0:T(1,128)}, u32[]{:S(2)}, u32[]{:S(2)}) collective-permute-start(f32[60,64,1]{1,2,0:T(1,128)} %copy.2917), channel_id=1, source_target_pairs={{1,0},{2,1},{3,2},{4,3},{5,4},{6,5},{7,6},{8,7},{9,8},{10,9},{11,1... | collective-permute-start | bytes 46088 | tf_op jit(solution)/shard_map/ppermute | solution.py:34
  259.2 22.5 %collective-permute-start.13 = (f32[60,1,128]{2,1,0:T(1,128)}, f32[60,1,128]{2,1,0:T(1,128)}, u32[]{:S(2)}, u32[]{:S(2)}) collective-permute-start(f32[60,1,128]{2,1,0:T(1,128)} %slice.1967), channel_id=1, source_target_pairs={{0,16},{16,32},{32,48},{48,64},{64,80},{80,96},{96,112},{1,17},{17... | collective-permute-start | bytes 92168 | tf_op jit(solution)/shard_map/ppermute | solution.py:34
  269.9 9.1 %collective-permute-start.15 = (f32[60,64,1]{1,2,0:T(1,128)}, f32[60,64,1]{1,2,0:T(1,128)}, u32[]{:S(2)}, u32[]{:S(2)}) collective-permute-start(f32[60,64,1]{1,2,0:T(1,128)} %copy.2919), channel_id=1, source_target_pairs={{0,1},{1,2},{2,3},{3,4},{4,5},{5,6},{6,7},{7,8},{8,9},{9,10},{10,1... | collective-permute-start | bytes 46088 | tf_op jit(solution)/shard_map/ppermute | solution.py:34
  293.3 11.1 %collective-permute-start.16 = (f32[60,1,128]{2,1,0:T(1,128)}, f32[60,1,128]{2,1,0:T(1,128)}, u32[]{:S(2)}, u32[]{:S(2)}) collective-permute-start(f32[60,1,128]{2,1,0:T(1,128)} %slice.2035), channel_id=1, source_target_pairs={{16,0},{32,16},{48,32},{64,48},{80,64},{96,80},{112,96},{17,1},{33... | collective-permute-start | bytes 92168 | tf_op jit(solution)/shard_map/ppermute | solution.py:34
  296.5 5.3 %collective-permute-start.18 = (f32[60,64,1]{1,2,0:T(1,128)}, f32[60,64,1]{1,2,0:T(1,128)}, u32[]{:S(2)}, u32[]{:S(2)}) collective-permute-start(f32[60,64,1]{1,2,0:T(1,128)} %copy.2921), channel_id=1, source_target_pairs={{1,0},{2,1},{3,2},{4,3},{5,4},{6,5},{7,6},{8,7},{9,8},{10,9},{11,1... | collective-permute-start | bytes 46088 | tf_op jit(solution)/shard_map/ppermute | solution.py:34
  311.5 22.5 %collective-permute-start.17 = (f32[60,1,128]{2,1,0:T(1,128)}, f32[60,1,128]{2,1,0:T(1,128)}, u32[]{:S(2)}, u32[]{:S(2)}) collective-permute-start(f32[60,1,128]{2,1,0:T(1,128)} %slice.2036), channel_id=1, source_target_pairs={{0,16},{16,32},{32,48},{48,64},{64,80},{80,96},{96,112},{1,17},{17... | collective-permute-start | bytes 92168 | tf_op jit(solution)/shard_map/ppermute | solution.py:34
  322.2 9.1 %collective-permute-start.19 = (f32[60,64,1]{1,2,0:T(1,128)}, f32[60,64,1]{1,2,0:T(1,128)}, u32[]{:S(2)}, u32[]{:S(2)}) collective-permute-start(f32[60,64,1]{1,2,0:T(1,128)} %copy.2923), channel_id=1, source_target_pairs={{0,1},{1,2},{2,3},{3,4},{4,5},{5,6},{6,7},{7,8},{8,9},{9,10},{10,1... | collective-permute-start | bytes 46088 | tf_op jit(solution)/shard_map/ppermute | solution.py:34
  345.7 11.1 %collective-permute-start.20 = (f32[60,1,128]{2,1,0:T(1,128)}, f32[60,1,128]{2,1,0:T(1,128)}, u32[]{:S(2)}, u32[]{:S(2)}) collective-permute-start(f32[60,1,128]{2,1,0:T(1,128)} %slice.2104), channel_id=1, source_target_pairs={{16,0},{32,16},{48,32},{64,48},{80,64},{96,80},{112,96},{17,1},{33... | collective-permute-start | bytes 92168 | tf_op jit(solution)/shard_map/ppermute | solution.py:34
  364.0 22.5 %collective-permute-start.22 = (f32[60,1,128]{2,1,0:T(1,128)}, f32[60,1,128]{2,1,0:T(1,128)}, u32[]{:S(2)}, u32[]{:S(2)}) collective-permute-start(f32[60,1,128]{2,1,0:T(1,128)} %slice.2107), channel_id=1, source_target_pairs={{0,16},{16,32},{32,48},{48,64},{64,80},{80,96},{96,112},{1,17},{17... | collective-permute-start | bytes 92168 | tf_op jit(solution)/shard_map/ppermute | solution.py:34
  374.7 9.1 %collective-permute-start.23 = (f32[60,64,1]{1,2,0:T(1,128)}, f32[60,64,1]{1,2,0:T(1,128)}, u32[]{:S(2)}, u32[]{:S(2)}) collective-permute-start(f32[60,64,1]{1,2,0:T(1,128)} %copy.2927), channel_id=1, source_target_pairs={{0,1},{1,2},{2,3},{3,4},{4,5},{5,6},{6,7},{7,8},{8,9},{9,10},{10,1... | collective-permute-start | bytes 46088 | tf_op jit(solution)/shard_map/ppermute | solution.py:34
  (83 other events, 160.9 us)
where the time goes:
time: 405 us; the launch traced here: 398 us
  local copies, waits for them, and re-layouts  160 us (40%)
  other arithmetic  88.6 us (22%)
  starting transfers between devices  80.3 us (20%)
  waiting for transfers between devices  40.1 us (10%)
  blocking collectives  24.6 us (6%)
  between operations  4.64 us (1%)
    ppermute x24, starting transfers between devices, passed_along(): return lax.ppermute(block, axis, route)  74.5 us
    ppermute x24, waiting for transfers between devices, passed_along(): return lax.ppermute(block, axis, route)  40.1 us
    unnamed x510, local copies, waits for them, and re-layouts  33.7 us
    sub x6, other arithmetic, per_device(): v_now = v_now - accel * (north_p - p_now)  33.2 us
    ppermute x12, local copies, waits for them, and re-layouts, passed_along(): return lax.ppermute(block, axis, route)  31.4 us
    sub x6, other arithmetic, column_part(): sectioned = p_old - spread * diverge  30.3 us
    slice x12, local copies, waits for them, and re-layouts, per_device(): south_rim = passed_along(v_now[:, :, -1:], 'gy', 1)  27.2 us
    all_gather x1, blocking collectives, per_device(): side_vals = lax.all_gather(sn_slab, 'gy', axis=4, tiled=True)  24.6 us
  transfers between devices with their start and end apart: 25, of which 6 were waited for; matrix products, arithmetic and copies ran while one was open for 29% of the time, Pallas kernels for 0%

commit v1 on v0

v1 whole, which is shorter than its diff:
```python
import functools

import jax
import jax.numpy as jnp
from jax import lax
from jax.experimental import pallas as pl
from jax.experimental.pallas import tpu as pltpu
from jax.sharding import PartitionSpec as PS

MESH = pl.DeviceIdType.MESH
STEPS = 6
GROUPS = 4
ORDER = (0, 3, 1, 2)
BAND = 5
F32 = jnp.float32


def kernel(ngx, ngy, nz, rx, ly,
           u_hbm, v_hbm, w_hbm, p_hbm, r_hbm, we_hbm, sn_hbm, rate_hbm,
           uo_hbm, vo_hbm, wo_hbm, po_hbm,
           P, E, S, W, G, U, V, R, RW, WEL, SNL, WPK, SPK, WEB, SNB, TT, BB, QQ,
           EB, RN, RS, EV, RV, SN, KK,
           lsem, osem, ssem, rsem, wssem, wrsem, sssem, srsem):
    gx = lax.axis_index("gx")
    gy = lax.axis_index("gy")
    rows = rx // GROUPS
    sy = ly // ngx
    sx = rx // ngy

    def load(i, src, dst):
        c = pltpu.make_async_copy(src, dst, lsem.at[i])
        c.start()
        return c

    l_we = load(5, we_hbm, WEL)
    l_sn = load(6, sn_hbm, SNL)
    l_r = load(4, r_hbm, R)
    l_rate = load(7, rate_hbm, RW)
    l_p = load(3, p_hbm, P.at[0, :, pl.ds(8, rx), :])
    l_u = load(0, u_hbm, U.at[:, pl.ds(8, rx), :])
    l_v = load(1, v_hbm, V)
    l_w = load(2, w_hbm, W)

    barrier = pltpu.get_barrier_semaphore()

    def peers(me, other, n):
        return (other != me) & (
            (other == me - 1) | (other == me + 1) | (other == 0) | (other == n - 1)
            | (me == 0) | (me == n - 1))

    count = jnp.int32(0)
    for k in range(ngx):
        ok = peers(gx, k, ngx)
        count = count + jnp.where(ok, 1, 0)

        @pl.when(ok)
        def _(k=k):
            pl.semaphore_signal(barrier, inc=1, device_id=(k, gy), device_id_type=MESH)
    for k in range(ngy):
        ok = peers(gy, k, ngy)
        count = count + jnp.where(ok, 1, 0)

        @pl.when(ok)
        def _(k=k):
            pl.semaphore_signal(barrier, inc=1, device_id=(gx, k), device_id_type=MESH)

    WPK[...] = jnp.zeros_like(WPK)
    SPK[...] = jnp.zeros_like(SPK)
    l_we.wait()
    l_sn.wait()
    for side in range(2):
        for i in range(3 * BAND):
            f, d = i // BAND, i % BAND
            lo = 0 if i < 8 else 64
            WPK[side, i % 8, :, lo:lo + nz] = WEL[side, f, d]
            SPK[side, i % 8, :, lo:lo + nz] = SNL[side, f, d]

    pl.semaphore_wait(barrier, count)

    def we_copy(side, k):
        dest = 0 if side == 0 else ngx - 1
        return pltpu.make_async_remote_copy(
            src_ref=WPK.at[side], dst_ref=WEB.at[k], send_sem=wssem.at[side],
            recv_sem=wrsem.at[k], device_id=(dest, gy), device_id_type=MESH)

    def sn_copy(side, k):
        dest = 0 if side == 0 else ngy - 1
        return pltpu.make_async_remote_copy(
            src_ref=SPK.at[side], dst_ref=SNB.at[k], send_sem=sssem.at[side],
            recv_sem=srsem.at[k], device_id=(gx, dest), device_id_type=MESH)

    for side in range(2):
        @pl.when(gx != (0 if side == 0 else ngx - 1))
        def _(side=side):
            we_copy(side, gx).start()

        @pl.when(gy != (0 if side == 0 else ngy - 1))
        def _(side=side):
            sn_copy(side, gy).start()

    l_r.wait()
    r_all = R[...]
    base = 1.0 + 2.0 * r_all

    def factor(z, prev):
        g = r_all / (base - r_all * prev)
        G[z] = g
        return g

    lax.fori_loop(0, nz, factor, jnp.zeros_like(r_all))

    l_rate.wait()
    l_p.wait()
    l_u.wait()
    l_v.wait()

    def field_row(f, x):
        if f == 0:
            return U.at[:, 8 + x, :]
        if f == 1:
            return V.at[:, x, :]
        return P.at[0, :, 8 + x, :]

    def blend_x(side):
        me = 0 if side == 0 else ngx - 1
        for k in range(ngx):
            if k == me:
                WEB[k] = WPK[side]
            else:
                we_copy(side, k).wait_recv()
        for i in range(8):
            for k in range(ngx):
                TT[k * sy:(k + 1) * sy, :] = WEB[k, i]
            turned = jnp.transpose(TT[...])
            for half in range(2):
                n = i + 8 * half
                if n >= 3 * BAND:
                    continue
                f, d = n // BAND, n % BAND
                x = d if side == 0 else rx - 1 - d
                rate = RW[x:x + 1, :].astype(F32)
                weight = jnp.maximum(rate - float(d), 0.0) / rate
                slab = turned[64 * half:64 * half + nz]
                row = field_row(f, x)
                old = row[...]
                row[...] = old + weight * (slab - old)

    def blend_y(side):
        me = 0 if side == 0 else ngy - 1
        for k in range(ngy):
            if k == me:
                SNB[k] = SPK[side]
            else:
                sn_copy(side, k).wait_recv()
        BB[...] = jnp.zeros_like(BB)
        TT[...] = jnp.zeros_like(TT)
        for i in range(8):
            for k in range(ngy):
                TT[k * sx:(k + 1) * sx, :] = SNB[k, i]
            turned = jnp.transpose(TT[...])
            for half in range(2):
                n = i + 8 * half
                if n >= 3 * BAND:
                    continue
                f, d = n // BAND, n % BAND
                dd = d if side == 0 else 7 - d
                BB[f, :, dd, :] = turned[64 * half:64 * half + 64]
        for f in range(3):
            for q in range(4):
                block = BB[f, 16 * q:16 * q + 16].reshape(128, 128)
                QQ[f, q] = jnp.transpose(block)[:rx]
        lane = lax.broadcasted_iota(jnp.int32, (rx, ly), 1).astype(F32)
        dist = lane if side == 0 else (ly - 1.0) - lane
        rate = RW[...].astype(F32)
        weight = jnp.maximum(rate - dist, 0.0) / rate

        def level(z, _):
            q = z // 16
            shift = (0 if side == 0 else 120) + 128 - 8 * (z % 16)
            shift = lax.rem(shift, 128)
            for f in range(3):
                slab = pltpu.roll(QQ[f, q], shift, 1)
                if f == 0:
                    dst = U.at[z, pl.ds(8, rx), :]
                elif f == 1:
                    dst = V.at[z]
                else:
                    dst = P.at[0, z, pl.ds(8, rx), :]
                old = dst[...]
                dst[...] = old + weight * (slab - old)
            return 0

        lax.fori_loop(0, nz, level, 0)

    for side in range(2):
        @pl.when(gx == (0 if side == 0 else ngx - 1))
        def _(side=side):
            blend_x(side)
    for side in range(2):
        @pl.when(gy == (0 if side == 0 else ngy - 1))
        def _(side=side):
            blend_y(side)

    pair = lax.broadcasted_iota(jnp.int32, (rows, ly), 1) // 2
    lane_r = lax.broadcasted_iota(jnp.int32, (rows, ly), 1)
    rim = (lane_r == 0) | (lane_r == ly - 1)

    def put(acc, value, z):
        return jnp.where(pair == z, pltpu.roll(value, lax.rem(2 * z + 1, 128), 1), acc)

    def own_rows(g):
        return pl.ds(8 + g * rows, rows)

    def all_rows(g):
        return pl.ds(g * rows, rows)

    def x_west(par):
        return pltpu.make_async_remote_copy(
            src_ref=P.at[par, :, pl.ds(8, 1), :], dst_ref=P.at[par, :, pl.ds(8 + rx, 1), :],
            send_sem=ssem.at[0, par], recv_sem=rsem.at[0, par],
            device_id=(gx - 1, gy), device_id_type=MESH)

    def x_east(par):
        return pltpu.make_async_remote_copy(
            src_ref=P.at[par, :, pl.ds(7 + rx, 1), :], dst_ref=P.at[par, :, pl.ds(7, 1), :],
            send_sem=ssem.at[1, par], recv_sem=rsem.at[1, par],
            device_id=(gx + 1, gy), device_id_type=MESH)

    def u_east():
        return pltpu.make_async_remote_copy(
            src_ref=U.at[:, pl.ds(7 + rx, 1), :], dst_ref=U.at[:, pl.ds(7, 1), :],
            send_sem=ssem.at[10, 0], recv_sem=rsem.at[10, 0],
            device_id=(gx + 1, gy), device_id_type=MESH)

    def y_north(par, g):
        return pltpu.make_async_remote_copy(
            src_ref=EB.at[par, all_rows(g)], dst_ref=RS.at[par, all_rows(g)],
            send_sem=ssem.at[2 + g, par], recv_sem=rsem.at[2 + g, par],
            device_id=(gx, gy + 1), device_id_type=MESH)

    def y_south(par, g):
        return pltpu.make_async_remote_copy(
            src_ref=EB.at[par, all_rows(g)], dst_ref=RN.at[par, all_rows(g)],
            send_sem=ssem.at[6 + g, par], recv_sem=rsem.at[6 + g, par],
            device_id=(gx, gy - 1), device_id_type=MESH)

    def v_north():
        return pltpu.make_async_remote_copy(
            src_ref=EV, dst_ref=RV,
            send_sem=ssem.at[11, 0], recv_sem=rsem.at[11, 0],
            device_id=(gx, gy + 1), device_id_type=MESH)

    has_w, has_e = gx > 0, gx < ngx - 1
    has_s, has_n = gy > 0, gy < ngy - 1

    def send_group(par, g):
        if g == 0:
            @pl.when(has_w)
            def _():
                x_west(par).start()

            @pl.when(jnp.logical_not(has_w))
            def _():
                P[par, :, 7, :] = P[par, :, 8, :]
        if g == GROUPS - 1:
            @pl.when(has_e)
            def _():
                x_east(par).start()

        @pl.when(has_n)
        def _():
            y_north(par, g).start()

        @pl.when(has_s)
        def _():
            y_south(par, g).start()

    def wait_group(par, g):
        if g == 0:
            @pl.when(has_w)
            def _():
                x_east(par).wait_recv()
                x_west(par).wait_send()
        if g == GROUPS - 1:
            @pl.when(has_e)
            def _():
                x_west(par).wait_recv()
                x_east(par).wait_send()

        @pl.when(has_n)
        def _():
            y_south(par, g).wait_recv()
            y_north(par, g).wait_send()

        @pl.when(has_s)
        def _():
            y_north(par, g).wait_recv()
            y_south(par, g).wait_send()

    @pl.when(jnp.logical_not(has_w))
    def _():
        U[:, 7, :] = jnp.zeros((nz, ly), F32)

    @pl.when(jnp.logical_not(has_e))
    def _():
        for par in range(2):
            P[par, :, 8 + rx, :] = jnp.zeros((nz, ly), F32)

    @pl.when(jnp.logical_not(has_n))
    def _():
        RN[...] = jnp.zeros_like(RN)

    @pl.when(jnp.logical_not(has_s))
    def _():
        RV[...] = jnp.zeros_like(RV)

    @pl.when(has_e)
    def _():
        u_east().start()

    for g in ORDER:
        def first(z, accs):
            acc_p, acc_v = accs
            return (put(acc_p, P[0, z, own_rows(g)], z), put(acc_v, V[z, all_rows(g)], z))

        none = jnp.zeros((rows, ly), F32)
        acc_p, acc_v = lax.fori_loop(0, nz, first, (none, none))
        EB[0, all_rows(g)] = acc_p
        EV[all_rows(g)] = acc_v
        send_group(0, g)

    @pl.when(has_n)
    def _():
        v_north().start()

    @pl.when(has_e)
    def _():
        u_east().wait_send()

    @pl.when(has_w)
    def _():
        u_east().wait_recv()

    @pl.when(has_n)
    def _():
        v_north().wait_send()

    @pl.when(has_s)
    def _():
        v_north().wait_recv()

    SN[...] = jnp.zeros_like(SN)
    S[:, rx, :] = jnp.zeros((nz, ly), F32)
    first_lane = lane_r == 0
    last_lane = lane_r == ly - 1
    for g in range(GROUPS):
        halo_v = RV[all_rows(g)]

        def divergence(z, _):
            u = U[z, own_rows(g)]
            uw = U[z, pl.ds(7 + g * rows, rows)]
            v = V[z, all_rows(g)]
            vs = jnp.where(first_lane, pltpu.roll(halo_v, lax.rem(128 - 2 * z, 128), 1),
                           pltpu.roll(v, 1, 1))
            E[z, all_rows(g)] = 0.3 * ((u - uw) + (v - vs))
            S[z, all_rows(g)] = jnp.zeros((rows, ly), F32)
            return 0

        lax.fori_loop(0, nz, divergence, 0)

    l_w.wait()

    even = lax.rem(lane_r, 2) == 0

    def corrections(cur, g):
        eb = EB[cur, all_rows(g)]
        rn = RN[cur, all_rows(g)]
        rs = jnp.where(has_s, RS[cur, all_rows(g)], pltpu.roll(eb, 127, 1))
        x = jnp.where(even, rs, rn) - eb
        SN[all_rows(g)] = SN[all_rows(g)] + rn
        return jnp.where(even, pltpu.roll(x, 127, 1), pltpu.roll(x, 1, 1))

    def forward(cur, nxt, g):
        r_rows = R[all_rows(g)]
        rinv = 1.0 / r_rows
        k_g = corrections(cur, g)

        def get_q(z):
            p = P[cur, z, own_rows(g)]
            pe = P[cur, z, pl.ds(9 + g * rows, rows)]
            pw = P[cur, z, pl.ds(7 + g * rows, rows)]
            ns = pltpu.roll(p, 1, 1) + pltpu.roll(p, 127, 1)
            k = jnp.where(rim, pltpu.roll(k_g, lax.rem(255 - 2 * z, 128), 1), 0.0)
            total = (pe + pw) + (ns + k)
            e = E[z, all_rows(g)] + 0.09 * (4.0 * p - total)
            E[z, all_rows(g)] = e
            S[z, all_rows(g)] = S[z, all_rows(g)] + p
            q = p - e
            P[nxt, z, own_rows(g)] = q
            return q

        def one(z, carry, last=False):
            q, dprev = carry
            if last:
                qn, diff = q, q
            else:
                qn = get_q(z + 1)
                diff = q - qn
            rhs = W[z, all_rows(g)] + 0.5 * diff
            d = G[z, all_rows(g)] * (rinv * rhs + dprev)
            W[z, all_rows(g)] = d
            return qn, d

        carry = (get_q(0), jnp.zeros((rows, ly), F32))
        unroll = 4
        head = (nz - 1) % unroll
        for z in range(head):
            carry = one(z, carry)

        def body(i, carry):
            for k in range(unroll):
                carry = one(head + i * unroll + k, carry)
            return carry

        carry = lax.fori_loop(0, (nz - 1) // unroll, body, carry)
        one(nz - 1, carry, last=True)

    def backward(nxt, g, edges):
        none = jnp.zeros((rows, ly), F32)

        def one(z, carry):
            w_up, h_up, acc = carry
            w = W[z, all_rows(g)] + G[z, all_rows(g)] * w_up
            W[z, all_rows(g)] = w
            h = 0.5 * w
            p = (P[nxt, z + 1, own_rows(g)] - h_up) + h
            P[nxt, z + 1, own_rows(g)] = p
            if edges:
                acc = put(acc, p, z + 1)
            return w, h, acc

        w_top = W[nz - 1, all_rows(g)]
        carry = (w_top, 0.5 * w_top, none)
        unroll = 4
        head = (nz - 1) % unroll
        for k in range(head):
            carry = one(nz - 2 - k, carry)

        def body(i, carry):
            for k in range(unroll):
                carry = one(nz - 2 - head - i * unroll - k, carry)
            return carry

        _, h_up, acc = lax.fori_loop(0, (nz - 1) // unroll, body, carry)
        p = P[nxt, 0, own_rows(g)] - h_up
        P[nxt, 0, own_rows(g)] = p
        if edges:
            EB[nxt, all_rows(g)] = put(acc, p, 0)

    def east_sum(cur):
        S[:, rx, :] = S[:, rx, :] + P[cur, :, 8 + rx, :]

    def step(s, _):
        cur = lax.rem(s, 2)
        nxt = 1 - cur
        for g in ORDER:
            wait_group(cur, g)
            if g == GROUPS - 1:
                east_sum(cur)
            forward(cur, nxt, g)
            backward(nxt, g, True)
            send_group(nxt, g)
        return 0

    lax.fori_loop(0, STEPS - 1, step, 0)

    cur = (STEPS - 1) % 2
    nxt = 1 - cur
    outs = []

    def store(i, src, dst):
        c = pltpu.make_async_copy(src, dst, osem.at[i])
        c.start()
        outs.append(c)

    for g in ORDER:
        wait_group(cur, g)
        if g == GROUPS - 1:
            east_sum(cur)
        forward(cur, nxt, g)
        backward(nxt, g, False)
        store(g, W.at[:, all_rows(g), :], wo_hbm.at[:, all_rows(g), :])
        store(4 + g, P.at[nxt, :, own_rows(g), :], po_hbm.at[:, all_rows(g), :])
    for g in range(GROUPS):
        halo = SN[all_rows(g)]

        def winds(z, _):
            t = S[z, all_rows(g)]
            te = S[z, pl.ds(g * rows + 1, rows)]
            tn = jnp.where(last_lane, pltpu.roll(halo, lax.rem(254 - 2 * z, 128), 1),
                           pltpu.roll(t, 127, 1))
            U[z, own_rows(g)] = U[z, own_rows(g)] - 0.3 * (te - t)
            V[z, all_rows(g)] = V[z, all_rows(g)] - 0.3 * (tn - t)
            return 0

        lax.fori_loop(0, nz, winds, 0)
        store(8 + g, U.at[:, own_rows(g), :], uo_hbm.at[:, all_rows(g), :])
        store(12 + g, V.at[:, all_rows(g), :], vo_hbm.at[:, all_rows(g), :])

    for side in range(2):
        @pl.when(gx != (0 if side == 0 else ngx - 1))
        def _(side=side):
            we_copy(side, gx).wait_send()

        @pl.when(gy != (0 if side == 0 else ngy - 1))
        def _(side=side):
            sn_copy(side, gy).wait_send()
    for c in outs:
        c.wait()


def per_device(ngx, ngy, u, v, w, p, r, we, sn, rate):
    nz, rx, ly = p.shape
    we = jnp.transpose(we, (0, 1, 3, 4, 2))
    sn = jnp.transpose(sn, (0, 1, 3, 4, 2))
    field = jax.ShapeDtypeStruct((nz, rx, ly), F32)
    vm = lambda *s: pltpu.VMEM(s, F32)
    any_ = pl.BlockSpec(memory_space=pl.ANY)
    dma = pltpu.SemaphoreType.DMA
    scratch = [
        vm(2, nz, rx + 16, ly), vm(nz, rx, ly), vm(nz, rx + 8, ly), vm(nz, rx, ly), vm(nz, rx, ly),
        vm(nz, rx + 8, ly), vm(nz, rx, ly), vm(rx, ly), pltpu.VMEM((rx, ly), jnp.int32),
        vm(2, 3, BAND, ly // ngx, nz), vm(2, 3, BAND, rx // ngy, nz),
        vm(2, 8, ly // ngx, 128), vm(2, 8, rx // ngy, 128),
        vm(ngx, 8, ly // ngx, 128), vm(ngy, 8, rx // ngy, 128),
        vm(128, 128), vm(3, 64, 8, 128), vm(3, 4, rx, 128),
        vm(2, rx, ly), vm(2, rx, ly), vm(2, rx, ly), vm(rx, ly), vm(rx, ly), vm(rx, ly), vm(rx, ly),
        dma((8,)), dma((16,)), dma((12, 2)), dma((12, 2)),
        dma((2,)), dma((ngx,)), dma((2,)), dma((ngy,)),
    ]
    return pl.pallas_call(
        functools.partial(kernel, ngx, ngy, nz, rx, ly),
        out_shape=(field,) * 4,
        in_specs=[any_] * 8,
        out_specs=(any_,) * 4,
        scratch_shapes=scratch,
        compiler_params=pltpu.CompilerParams(collective_id=0, has_side_effects=True,
                                             vmem_limit_bytes=48 * 1024 * 1024),
    )(u, v, w, p, r, we, sn, rate)


def solution(mesh):
    ngx, ngy = mesh.shape["gx"], mesh.shape["gy"]
    grid = PS(None, "gx", "gy")
    return jax.shard_map(
        functools.partial(per_device, ngx, ngy),
        mesh=mesh,
        in_specs=(grid,) * 4 + (
            PS("gx", "gy"),
            PS(None, None, None, None, ("gy", "gx")),
            PS(None, None, None, None, ("gx", "gy")),
            PS("gx", "gy"),
        ),
        out_specs=(grid,) * 4,
        check_vma=False,
    )
```

time: 405 us -> 224 us (0.55)
  the two profiles are of different devices: /device:TPU:88 before, /device:TPU:32 now
where the time goes in v1:
time: 224 us; the launch traced here: 221 us
  Pallas kernels  210 us (94%)
  local copies, waits for them, and re-layouts  10.3 us (5%)
    pallas_call x1, Pallas kernels, per_device(): pl.pallas_call(functools.partial(kernel, ngx, ngy, nz, rx, ly), out_shape...  210 us
    unnamed x16, local copies, waits for them, and re-layouts  10.3 us

profile of v1, /device:TPU:32, one launch (start us, length us, event | category | flops | bytes accessed | tf_op | source)
XLA Modules:
  0.0 221.5 jit_solution(9997025985185818892)
XLA Ops:
  0.6 0.0 copy-start
  0.6 0.9 copy-done
  1.6 0.0 copy-start.1
  1.6 0.8 copy-done.1
  2.4 0.0 copy-start.2
  2.4 0.8 copy-done.2
  3.2 0.0 copy-start.3
  3.2 0.8 copy-done.3
  3.9 210.5 %shard_map.111 = (f32[60,64,128]{2,1,0:T(8,128)S(1)}, f32[60,64,128]{2,1,0:T(8,128)S(1)}, f32[60,64,128]{2,1,0:T(8,128)}, f32[60,64,128]{2,1,0:T(8,128)}) custom-call(f32[60,64,128]{2,1,0:T(8,128)} %u_hbm.1, f32[60,64,128]{2,1,0:T(8,128)} %v_hbm.1, f32[60,64,128]{2,1,0:T(8,128)} %w_hbm.1, f32[60,64,128]{2,1,0:T(8,128)} %p_hbm.1, f32[64,128]{1,0:T(8,128)S(1)} %copy-done.2, ...), custom_call_target="tpu_custom_call" | custom-call | tf_op jit(solution)/shard_map/pallas_call | solution.py:541
  214.4 1.3 copy.16
  215.7 0.0 copy-start.5
  215.7 1.3 copy.17
  217.0 1.0 copy-done.5
  218.0 0.0 copy-start.4
  218.0 1.3 copy.18
  219.2 1.0 copy-done.4
  220.2 1.3 copy.19
Async XLA Ops:
  0.6 0.9 copy-start
  1.6 0.8 copy-start.1
  2.4 0.8 copy-start.2
  3.2 0.8 copy-start.3
  215.7 2.3 %copy-start.5 = (f32[60,64,128]{2,1,0:T(8,128)S(1)}, f32[60,64,128]{2,1,0:T(8,128)}, u32[]{:S(2)}) copy-start(f32[60,64,128]{2,1,0:T(8,128)} %get-tuple-element.10) | copy-start | bytes 5898244
  218.0 2.3 %copy-start.4 = (f32[60,64,128]{2,1,0:T(8,128)S(1)}, f32[60,64,128]{2,1,0:T(8,128)}, u32[]{:S(2)}) copy-start(f32[60,64,128]{2,1,0:T(8,128)} %get-tuple-element.11) | copy-start | bytes 5898244

commit v2 on v1

--- a/solution.py
+++ b/solution.py
@@ -10,7 +10,6 @@
 MESH = pl.DeviceIdType.MESH
 STEPS = 6
 GROUPS = 4
-ORDER = (0, 3, 1, 2)
 BAND = 5
 F32 = jnp.float32
 
@@ -18,9 +17,10 @@
 def kernel(ngx, ngy, nz, rx, ly,
            u_hbm, v_hbm, w_hbm, p_hbm, r_hbm, we_hbm, sn_hbm, rate_hbm,
            uo_hbm, vo_hbm, wo_hbm, po_hbm,
-           P, E, S, W, G, U, V, R, RW, WEL, SNL, WPK, SPK, WEB, SNB, TT, BB, QQ,
+           PA, PB, E, S, W, G, U, V, R, RW, WEL, SNL, WPK, SPK, WEB, SNB, TT, BB, QQ,
            EB, RN, RS, EV, RV, SN, KK,
            lsem, osem, ssem, rsem, wssem, wrsem, sssem, srsem):
+    P = (PA, PB)
     gx = lax.axis_index("gx")
     gy = lax.axis_index("gy")
     rows = rx // GROUPS
@@ -36,7 +36,7 @@
     l_sn = load(6, sn_hbm, SNL)
     l_r = load(4, r_hbm, R)
     l_rate = load(7, rate_hbm, RW)
-    l_p = load(3, p_hbm, P.at[0, :, pl.ds(8, rx), :])
+    l_p = load(3, p_hbm, PA.at[:, pl.ds(8, rx), :])
     l_u = load(0, u_hbm, U.at[:, pl.ds(8, rx), :])
     l_v = load(1, v_hbm, V)
     l_w = load(2, w_hbm, W)
@@ -119,7 +119,7 @@
             return U.at[:, 8 + x, :]
         if f == 1:
             return V.at[:, x, :]
-        return P.at[0, :, 8 + x, :]
+        return PA.at[:, 8 + x, :]
 
     def blend_x(side):
         me = 0 if side == 0 else ngx - 1
@@ -169,28 +169,28 @@
             for q in range(4):
                 block = BB[f, 16 * q:16 * q + 16].reshape(128, 128)
                 QQ[f, q] = jnp.transpose(block)[:rx]
-        lane = lax.broadcasted_iota(jnp.int32, (rx, ly), 1).astype(F32)
+        lane = lax.broadcasted_iota(jnp.int32, (rows, ly), 1).astype(F32)
         dist = lane if side == 0 else (ly - 1.0) - lane
-        rate = RW[...].astype(F32)
-        weight = jnp.maximum(rate - dist, 0.0) / rate
-
-        def level(z, _):
-            q = z // 16
-            shift = (0 if side == 0 else 120) + 128 - 8 * (z % 16)
-            shift = lax.rem(shift, 128)
+
+        def part(g, _):
+            at = pl.multiple_of(g * rows, 8)
+            rate = RW[pl.ds(at, rows)].astype(F32)
+            weight = jnp.maximum(rate - dist, 0.0) / rate
             for f in range(3):
-                slab = pltpu.roll(QQ[f, q], shift, 1)
-                if f == 0:
-                    dst = U.at[z, pl.ds(8, rx), :]
-                elif f == 1:
-                    dst = V.at[z]
-                else:
-                    dst = P.at[0, z, pl.ds(8, rx), :]
-                old = dst[...]
-                dst[...] = old + weight * (slab - old)
+                for z in range(nz):
+                    shift = ((0 if side == 0 else 120) + 128 - 8 * (z % 16)) % 128
+                    slab = pltpu.roll(QQ[f, z // 16, pl.ds(at, rows)], shift, 1)
+                    if f == 0:
+                        dst = U.at[z, pl.ds(at + 8, rows), :]
+                    elif f == 1:
+                        dst = V.at[z, pl.ds(at, rows), :]
+                    else:
+                        dst = PA.at[z, pl.ds(at + 8, rows), :]
+                    old = dst[...]
+                    dst[...] = old + weight * (slab - old)
             return 0
 
-        lax.fori_loop(0, nz, level, 0)
+        lax.fori_loop(0, GROUPS, part, 0)
 
     for side in range(2):
         @pl.when(gx == (0 if side == 0 else ngx - 1))
@@ -206,23 +206,26 @@
     rim = (lane_r == 0) | (lane_r == ly - 1)
 
     def put(acc, value, z):
-        return jnp.where(pair == z, pltpu.roll(value, lax.rem(2 * z + 1, 128), 1), acc)
+        return jnp.where(pair == z, pltpu.roll(value, (2 * z + 1) % 128, 1), acc)
 
     def own_rows(g):
-        return pl.ds(8 + g * rows, rows)
+        return pl.ds(pl.multiple_of(8 + g * rows, 8), rows)
 
     def all_rows(g):
-        return pl.ds(g * rows, rows)
+        return pl.ds(pl.multiple_of(g * rows, 8), rows)
+
+    def in_order(i):
+        return jnp.where(i == 0, 0, jnp.where(i == 1, GROUPS - 1, i - 1))
 
     def x_west(par):
         return pltpu.make_async_remote_copy(
-            src_ref=P.at[par, :, pl.ds(8, 1), :], dst_ref=P.at[par, :, pl.ds(8 + rx, 1), :],
+            src_ref=P[par].at[:, pl.ds(8, 1), :], dst_ref=P[par].at[:, pl.ds(8 + rx, 1), :],
             send_sem=ssem.at[0, par], recv_sem=rsem.at[0, par],
             device_id=(gx - 1, gy), device_id_type=MESH)
 
     def x_east(par):
         return pltpu.make_async_remote_copy(
-            src_ref=P.at[par, :, pl.ds(7 + rx, 1), :], dst_ref=P.at[par, :, pl.ds(7, 1), :],
+            src_ref=P[par].at[:, pl.ds(7 + rx, 1), :], dst_ref=P[par].at[:, pl.ds(7, 1), :],
             send_sem=ssem.at[1, par], recv_sem=rsem.at[1, par],
             device_id=(gx + 1, gy), device_id_type=MESH)
 
@@ -254,18 +257,17 @@
     has_s, has_n = gy > 0, gy < ngy - 1
 
     def send_group(par, g):
-        if g == 0:
-            @pl.when(has_w)
-            def _():
-                x_west(par).start()
-
-            @pl.when(jnp.logical_not(has_w))
-            def _():
-                P[par, :, 7, :] = P[par, :, 8, :]
-        if g == GROUPS - 1:
-            @pl.when(has_e)
-            def _():
-                x_east(par).start()
+        @pl.when((g == 0) & has_w)
+        def _():
+            x_west(par).start()
+
+        @pl.when((g == 0) & jnp.logical_not(has_w))
+        def _():
+            P[par][:, 7, :] = P[par][:, 8, :]
+
+        @pl.when((g == GROUPS - 1) & has_e)
+        def _():
+            x_east(par).start()
 
         @pl.when(has_n)
         def _():
@@ -276,16 +278,19 @@
             y_south(par, g).start()
 
     def wait_group(par, g):
-        if g == 0:
-            @pl.when(has_w)
-            def _():
-                x_east(par).wait_recv()
-                x_west(par).wait_send()
-        if g == GROUPS - 1:
-            @pl.when(has_e)
-            def _():
-                x_west(par).wait_recv()
-                x_east(par).wait_send()
+        @pl.when((g == 0) & has_w)
+        def _():
+            x_east(par).wait_recv()
+            x_west(par).wait_send()
+
+        @pl.when((g == GROUPS - 1) & has_e)
+        def _():
+            x_west(par).wait_recv()
+            x_east(par).wait_send()
+
+        @pl.when(g == GROUPS - 1)
+        def _():
+            S[:, rx, :] = S[:, rx, :] + P[par][:, 8 + rx, :]
 
         @pl.when(has_n)
         def _():
@@ -304,7 +309,7 @@
     @pl.when(jnp.logical_not(has_e))
     def _():
         for par in range(2):
-            P[par, :, 8 + rx, :] = jnp.zeros((nz, ly), F32)
+            P[par][:, 8 + rx, :] = jnp.zeros((nz, ly), F32)
 
     @pl.when(jnp.logical_not(has_n))
     def _():
@@ -318,16 +323,19 @@
     def _():
         u_east().start()
 
-    for g in ORDER:
-        def first(z, accs):
-            acc_p, acc_v = accs
-            return (put(acc_p, P[0, z, own_rows(g)], z), put(acc_v, V[z, all_rows(g)], z))
-
-        none = jnp.zeros((rows, ly), F32)
-        acc_p, acc_v = lax.fori_loop(0, nz, first, (none, none))
+    def first(i, _):
+        g = in_order(i)
+        acc_p = jnp.zeros((rows, ly), F32)
+        acc_v = jnp.zeros((rows, ly), F32)
+        for z in range(nz):
+            acc_p = put(acc_p, PA[z, own_rows(g)], z)
+            acc_v = put(acc_v, V[z, all_rows(g)], z)
         EB[0, all_rows(g)] = acc_p
         EV[all_rows(g)] = acc_v
         send_group(0, g)
+        return 0
+
+    lax.fori_loop(0, GROUPS, first, 0)
 
     @pl.when(has_n)
     def _():
@@ -353,20 +361,20 @@
     S[:, rx, :] = jnp.zeros((nz, ly), F32)
     first_lane = lane_r == 0
     last_lane = lane_r == ly - 1
-    for g in range(GROUPS):
+
+    def divergence(g, _):
         halo_v = RV[all_rows(g)]
-
-        def divergence(z, _):
+        for z in range(nz):
             u = U[z, own_rows(g)]
             uw = U[z, pl.ds(7 + g * rows, rows)]
             v = V[z, all_rows(g)]
-            vs = jnp.where(first_lane, pltpu.roll(halo_v, lax.rem(128 - 2 * z, 128), 1),
+            vs = jnp.where(first_lane, pltpu.roll(halo_v, (128 - 2 * z) % 128, 1),
                            pltpu.roll(v, 1, 1))
             E[z, all_rows(g)] = 0.3 * ((u - uw) + (v - vs))
             S[z, all_rows(g)] = jnp.zeros((rows, ly), F32)
-            return 0
-
-        lax.fori_loop(0, nz, divergence, 0)
+        return 0
+
+    lax.fori_loop(0, GROUPS, divergence, 0)
 
     l_w.wait()
 
@@ -381,131 +389,99 @@
         return jnp.where(even, pltpu.roll(x, 127, 1), pltpu.roll(x, 1, 1))
 
     def forward(cur, nxt, g):
-        r_rows = R[all_rows(g)]
-        rinv = 1.0 / r_rows
+        rinv = 1.0 / R[all_rows(g)]
         k_g = corrections(cur, g)
 
         def get_q(z):
-            p = P[cur, z, own_rows(g)]
-            pe = P[cur, z, pl.ds(9 + g * rows, rows)]
-            pw = P[cur, z, pl.ds(7 + g * rows, rows)]
+            p = P[cur][z, own_rows(g)]
+            pe = P[cur][z, pl.ds(9 + g * rows, rows)]
+            pw = P[cur][z, pl.ds(7 + g * rows, rows)]
             ns = pltpu.roll(p, 1, 1) + pltpu.roll(p, 127, 1)
-            k = jnp.where(rim, pltpu.roll(k_g, lax.rem(255 - 2 * z, 128), 1), 0.0)
+            k = jnp.where(rim, pltpu.roll(k_g, (255 - 2 * z) % 128, 1), 0.0)
             total = (pe + pw) + (ns + k)
             e = E[z, all_rows(g)] + 0.09 * (4.0 * p - total)
             E[z, all_rows(g)] = e
             S[z, all_rows(g)] = S[z, all_rows(g)] + p
             q = p - e
-            P[nxt, z, own_rows(g)] = q
+            P[nxt][z, own_rows(g)] = q
             return q
 
-        def one(z, carry, last=False):
-            q, dprev = carry
-            if last:
-                qn, diff = q, q
-            else:
-                qn = get_q(z + 1)
-                diff = q - qn
+        q, d = get_q(0), jnp.zeros((rows, ly), F32)
+        for z in range(nz):
+            qn = get_q(z + 1) if z < nz - 1 else None
+            diff = q - qn if z < nz - 1 else q
             rhs = W[z, all_rows(g)] + 0.5 * diff
-            d = G[z, all_rows(g)] * (rinv * rhs + dprev)
+            d = G[z, all_rows(g)] * (rinv * rhs + d)
             W[z, all_rows(g)] = d
-            return qn, d
-
-        carry = (get_q(0), jnp.zeros((rows, ly), F32))
-        unroll = 4
-        head = (nz - 1) % unroll
-        for z in range(head):
-            carry = one(z, carry)
-
-        def body(i, carry):
-            for k in range(unroll):
-                carry = one(head + i * unroll + k, carry)
-            return carry
-
-        carry = lax.fori_loop(0, (nz - 1) // unroll, body, carry)
-        one(nz - 1, carry, last=True)
+            q = qn
 
     def backward(nxt, g, edges):
-        none = jnp.zeros((rows, ly), F32)
-
-        def one(z, carry):
-            w_up, h_up, acc = carry
-            w = W[z, all_rows(g)] + G[z, all_rows(g)] * w_up
-            W[z, all_rows(g)] = w
-            h = 0.5 * w
-            p = (P[nxt, z + 1, own_rows(g)] - h_up) + h
-            P[nxt, z + 1, own_rows(g)] = p
+        acc = jnp.zeros((rows, ly), F32)
+        w = W[nz - 1, all_rows(g)]
+        h = 0.5 * w
+        for z in range(nz - 2, -2, -1):
+            p = P[nxt][z + 1, own_rows(g)] - h
+            if z >= 0:
+                w = W[z, all_rows(g)] + G[z, all_rows(g)] * w
+                W[z, all_rows(g)] = w
+                h = 0.5 * w
+                p = p + h
+            P[nxt][z + 1, own_rows(g)] = p
             if edges:
                 acc = put(acc, p, z + 1)
-            return w, h, acc
-
-        w_top = W[nz - 1, all_rows(g)]
-        carry = (w_top, 0.5 * w_top, none)
-        unroll = 4
-        head = (nz - 1) % unroll
-        for k in range(head):
-            carry = one(nz - 2 - k, carry)
-
-        def body(i, carry):
-            for k in range(unroll):
-                carry = one(nz - 2 - head - i * unroll - k, carry)
-            return carry
-
-        _, h_up, acc = lax.fori_loop(0, (nz - 1) // unroll, body, carry)
-        p = P[nxt, 0, own_rows(g)] - h_up
-        P[nxt, 0, own_rows(g)] = p
         if edges:
-            EB[nxt, all_rows(g)] = put(acc, p, 0)
-
-    def east_sum(cur):
-        S[:, rx, :] = S[:, rx, :] + P[cur, :, 8 + rx, :]
-
-    def step(s, _):
-        cur = lax.rem(s, 2)
-        nxt = 1 - cur
-        for g in ORDER:
+            EB[nxt, all_rows(g)] = acc
+
+    def step(cur, nxt):
+        def part(i, _):
+            g = in_order(i)
             wait_group(cur, g)
-            if g == GROUPS - 1:
-                east_sum(cur)
             forward(cur, nxt, g)
             backward(nxt, g, True)
             send_group(nxt, g)
+            return 0
+
+        lax.fori_loop(0, GROUPS, part, 0)
+
+    def two_steps(i, _):
+        step(0, 1)
+        step(1, 0)
         return 0
 
-    lax.fori_loop(0, STEPS - 1, step, 0)
-
-    cur = (STEPS - 1) % 2
-    nxt = 1 - cur
-    outs = []
-
-    def store(i, src, dst):
-        c = pltpu.make_async_copy(src, dst, osem.at[i])
-        c.start()
-        outs.append(c)
-
-    for g in ORDER:
-        wait_group(cur, g)
-        if g == GROUPS - 1:
-            east_sum(cur)
-        forward(cur, nxt, g)
-        backward(nxt, g, False)
-        store(g, W.at[:, all_rows(g), :], wo_hbm.at[:, all_rows(g), :])
-        store(4 + g, P.at[nxt, :, own_rows(g), :], po_hbm.at[:, all_rows(g), :])
-    for g in range(GROUPS):
+    lax.fori_loop(0, (STEPS - 2) // 2, two_steps, 0)
+    step(0, 1)
+
+    def stores(g, which):
+        to = lambda ref: ref.at[:, all_rows(g), :]
+        pairs = ((W.at[:, all_rows(g), :], to(wo_hbm)), (PA.at[:, own_rows(g), :], to(po_hbm)),
+                 (U.at[:, own_rows(g), :], to(uo_hbm)), (V.at[:, all_rows(g), :], to(vo_hbm)))
+        return [pltpu.make_async_copy(*pairs[k], osem.at[k, g]) for k in which]
+
+    def last(i, _):
+        g = in_order(i)
+        wait_group(1, g)
+        forward(1, 0, g)
+        backward(0, g, False)
+        for c in stores(g, (0, 1)):
+            c.start()
+        return 0
+
+    lax.fori_loop(0, GROUPS, last, 0)
+
+    def winds(g, _):
         halo = SN[all_rows(g)]
-
-        def winds(z, _):
+        for z in range(nz):
             t = S[z, all_rows(g)]
             te = S[z, pl.ds(g * rows + 1, rows)]
-            tn = jnp.where(last_lane, pltpu.roll(halo, lax.rem(254 - 2 * z, 128), 1),
+            tn = jnp.where(last_lane, pltpu.roll(halo, (254 - 2 * z) % 128, 1),
                            pltpu.roll(t, 127, 1))
             U[z, own_rows(g)] = U[z, own_rows(g)] - 0.3 * (te - t)
             V[z, all_rows(g)] = V[z, all_rows(g)] - 0.3 * (tn - t)
-            return 0
-
-        lax.fori_loop(0, nz, winds, 0)
-        store(8 + g, U.at[:, own_rows(g), :], uo_hbm.at[:, all_rows(g), :])
-        store(12 + g, V.at[:, all_rows(g), :], vo_hbm.at[:, all_rows(g), :])
+        for c in stores(g, (2, 3)):
+            c.start()
+        return 0
+
+    lax.fori_loop(0, GROUPS, winds, 0)
 
     for side in range(2):
         @pl.when(gx != (0 if side == 0 else ngx - 1))
@@ -515,8 +491,9 @@
         @pl.when(gy != (0 if side == 0 else ngy - 1))
         def _(side=side):
             sn_copy(side, gy).wait_send()
-    for c in outs:
-        c.wait()
+    for g in range(GROUPS):
+        for c in stores(g, range(4)):
+            c.wait()
 
 
 def per_device(ngx, ngy, u, v, w, p, r, we, sn, rate):
@@ -528,14 +505,14 @@
     any_ = pl.BlockSpec(memory_space=pl.ANY)
     dma = pltpu.SemaphoreType.DMA
     scratch = [
-        vm(2, nz, rx + 16, ly), vm(nz, rx, ly), vm(nz, rx + 8, ly), vm(nz, rx, ly), vm(nz, rx, ly),
+        vm(nz, rx + 16, ly), vm(nz, rx + 16, ly), vm(nz, rx, ly), vm(nz, rx + 8, ly), vm(nz, rx, ly), vm(nz, rx, ly),
         vm(nz, rx + 8, ly), vm(nz, rx, ly), vm(rx, ly), pltpu.VMEM((rx, ly), jnp.int32),
         vm(2, 3, BAND, ly // ngx, nz), vm(2, 3, BAND, rx // ngy, nz),
         vm(2, 8, ly // ngx, 128), vm(2, 8, rx // ngy, 128),
         vm(ngx, 8, ly // ngx, 128), vm(ngy, 8, rx // ngy, 128),
         vm(128, 128), vm(3, 64, 8, 128), vm(3, 4, rx, 128),
         vm(2, rx, ly), vm(2, rx, ly), vm(2, rx, ly), vm(rx, ly), vm(rx, ly), vm(rx, ly), vm(rx, ly),
-        dma((8,)), dma((16,)), dma((12, 2)), dma((12, 2)),
+        dma((8,)), dma((4, GROUPS)), dma((12, 2)), dma((12, 2)),
         dma((2,)), dma((ngx,)), dma((2,)), dma((ngy,)),
     ]
     return pl.pallas_call(
@@ -545,7 +522,7 @@
         out_specs=(any_,) * 4,
         scratch_shapes=scratch,
         compiler_params=pltpu.CompilerParams(collective_id=0, has_side_effects=True,
-                                             vmem_limit_bytes=48 * 1024 * 1024),
+                                             vmem_limit_bytes=63 * 1024 * 1024),
     )(u, v, w, p, r, we, sn, rate)
 
 

time: 224 us -> 60.1 us (0.27); the launches traced: 221 us -> 59.9 us
  Pallas kernels: 210 us -> 50.3 us
    pallas_call x1, Pallas kernels: 210 us -> 50.3 us  [per_device(): pl.pallas_call(functools.partial(kernel, ngx, ngy, nz, rx, ly), out_shape...]
    unnamed x16 -> x10, local copies, waits for them, and re-layouts: 10.3 us -> 8.97 us
where the time goes in v2:
time: 60.1 us; the launch traced here: 59.9 us
  Pallas kernels  50.3 us (84%)
  local copies, waits for them, and re-layouts  8.97 us (15%)
  between operations  0.65 us (1%)
    pallas_call x1, Pallas kernels, per_device(): pl.pallas_call(functools.partial(kernel, ngx, ngy, nz, rx, ly), out_shape...  50.3 us
    unnamed x10, local copies, waits for them, and re-layouts  8.97 us

profile of v2, /device:TPU:32, one launch (start us, length us, event | category | flops | bytes accessed | tf_op | source)
XLA Modules:
  0.0 59.9 jit_solution(6519714886484633783)
XLA Ops:
  0.6 50.3 %shard_map.111 = (f32[60,64,128]{2,1,0:T(8,128)}, f32[60,64,128]{2,1,0:T(8,128)}, f32[60,64,128]{2,1,0:T(8,128)}, f32[60,64,128]{2,1,0:T(8,128)}) custom-call(f32[60,64,128]{2,1,0:T(8,128)} %u_hbm.1, f32[60,64,128]{2,1,0:T(8,128)} %v_hbm.1, f32[60,64,128]{2,1,0:T(8,128)} %w_hbm.1, f32[60,64,128]{2,1,0:T(8,128)} %p_hbm.1, f32[64,128]{1,0:T(8,128)} %r_hbm.1, ...), custom_call_target="tpu_custom_call" | custom-call | tf_op jit(solution)/shard_map/pallas_call | solution.py:518
  50.9 0.0 copy-start.2
  50.9 3.2 %copy.16 = f32[60,64,128]{2,1,0:T(8,128)} copy(f32[60,64,128]{2,1,0:T(8,128)} %get-tuple-element.8) | data formatting | bytes 3932160
  54.1 0.0 copy-done.2
  54.1 0.0 copy-start.1
  54.1 1.3 %copy.17 = f32[60,64,128]{2,1,0:T(8,128)} copy(f32[60,64,128]{2,1,0:T(8,128)S(1)} %copy-done.2) | data formatting | bytes 3932160
  55.4 1.0 %copy-done.1 = f32[60,64,128]{2,1,0:T(8,128)S(1)} copy-done((f32[60,64,128]{2,1,0:T(8,128)S(1)}, f32[60,64,128]{2,1,0:T(8,128)}, u32[]{:S(2)}) %copy-start.1) | copy-done | bytes 1966104
  56.3 0.0 copy-start
  56.4 1.3 %copy.18 = f32[60,64,128]{2,1,0:T(8,128)} copy(f32[60,64,128]{2,1,0:T(8,128)S(1)} %copy-done.1) | data formatting | bytes 3932160
  57.6 1.0 %copy-done = f32[60,64,128]{2,1,0:T(8,128)S(1)} copy-done((f32[60,64,128]{2,1,0:T(8,128)S(1)}, f32[60,64,128]{2,1,0:T(8,128)}, u32[]{:S(2)}) %copy-start) | copy-done | bytes 1966104
  58.6 1.3 %copy.19 = f32[60,64,128]{2,1,0:T(8,128)} copy(f32[60,64,128]{2,1,0:T(8,128)S(1)} %copy-done) | data formatting | bytes 3932160
Async XLA Ops:
  50.9 3.2 %copy-start.2 = (f32[60,64,128]{2,1,0:T(8,128)S(1)}, f32[60,64,128]{2,1,0:T(8,128)}, u32[]{:S(2)}) copy-start(f32[60,64,128]{2,1,0:T(8,128)} %get-tuple-element.9) | copy-start | bytes 5898244
  54.1 2.3 %copy-start.1 = (f32[60,64,128]{2,1,0:T(8,128)S(1)}, f32[60,64,128]{2,1,0:T(8,128)}, u32[]{:S(2)}) copy-start(f32[60,64,128]{2,1,0:T(8,128)} %get-tuple-element.10) | copy-start | bytes 5898244
  56.3 2.3 %copy-start = (f32[60,64,128]{2,1,0:T(8,128)S(1)}, f32[60,64,128]{2,1,0:T(8,128)}, u32[]{:S(2)}) copy-start(f32[60,64,128]{2,1,0:T(8,128)} %get-tuple-element.11) | copy-start | bytes 5898244

commit v3 on v2

--- a/solution.py
+++ b/solution.py
@@ -16,13 +16,15 @@
 
 def kernel(ngx, ngy, nz, rx, ly,
            u_hbm, v_hbm, w_hbm, p_hbm, r_hbm, we_hbm, sn_hbm, rate_hbm,
-           uo_hbm, vo_hbm, wo_hbm, po_hbm,
-           PA, PB, E, S, W, G, U, V, R, RW, WEL, SNL, WPK, SPK, WEB, SNB, TT, BB, QQ,
-           EB, RN, RS, EV, RV, SN, KK,
-           lsem, osem, ssem, rsem, wssem, wrsem, sssem, srsem):
+           W, PA, U, V, S, SN,
+           PB, E, G, R, RW, WEL, SNL, WPK, SPK, WEB, SNB, TT, BB, BN, QQ, FO,
+           QX, EB, ES, RN, RS, EV, RV,
+           lsem, ssem, rsem, wssem, wrsem, sssem, srsem):
     P = (PA, PB)
     gx = lax.axis_index("gx")
     gy = lax.axis_index("gy")
+    has_w, has_e = gx > 0, gx < ngx - 1
+    has_s, has_n = gy > 0, gy < ngy - 1
     rows = rx // GROUPS
     sy = ly // ngx
     sx = rx // ngy
@@ -65,7 +67,9 @@
             pl.semaphore_signal(barrier, inc=1, device_id=(gx, k), device_id_type=MESH)
 
     WPK[...] = jnp.zeros_like(WPK)
-    SPK[...] = jnp.zeros_like(SPK)
+    BB[...] = jnp.zeros_like(BB)
+    BN[...] = jnp.zeros_like(BN)
+    TT[...] = jnp.zeros_like(TT)
     l_we.wait()
     l_sn.wait()
     for side in range(2):
@@ -73,7 +77,36 @@
             f, d = i // BAND, i % BAND
             lo = 0 if i < 8 else 64
             WPK[side, i % 8, :, lo:lo + nz] = WEL[side, f, d]
-            SPK[side, i % 8, :, lo:lo + nz] = SNL[side, f, d]
+
+    wide = 6 * sx
+    per = 128 // wide
+    for lot in range(0, BAND, per):
+        for d in range(lot, min(lot + per, BAND)):
+            for side in range(2):
+                for f in range(3):
+                    at = (d - lot) * wide + (side * 3 + f) * sx
+                    TT[at:at + sx, 0:nz] = SNL[side, f, d]
+        turned = jnp.transpose(TT[...])[:64]
+        for d in range(lot, min(lot + per, BAND)):
+            shift = (128 - (d - lot) * wide) % 128
+            moved = pltpu.roll(turned, shift, 1) if shift else turned
+            BB[:, d, :] = moved
+            BN[:, 7 - d, :] = moved
+    for q in range(4):
+        for side, ref in enumerate((BB, BN)):
+            block = jnp.transpose(ref[16 * q:16 * q + 16].reshape(128, 128))
+            SPK[side, q * 3 * sx:(q + 1) * 3 * sx, :] = block[side * 3 * sx:(side + 1) * 3 * sx]
+
+    l_r.wait()
+    r_all = R[...]
+    base = 1.0 + 2.0 * r_all
+
+    def factor(z, prev):
+        g = r_all / (base - r_all * prev)
+        G[z] = g
+        return g
+
+    lax.fori_loop(0, nz, factor, jnp.zeros_like(r_all))
 
     pl.semaphore_wait(barrier, count)
 
@@ -98,28 +131,27 @@
         def _(side=side):
             sn_copy(side, gy).start()
 
-    l_r.wait()
-    r_all = R[...]
-    base = 1.0 + 2.0 * r_all
-
-    def factor(z, prev):
-        g = r_all / (base - r_all * prev)
-        G[z] = g
-        return g
-
-    lax.fori_loop(0, nz, factor, jnp.zeros_like(r_all))
-
     l_rate.wait()
     l_p.wait()
     l_u.wait()
     l_v.wait()
 
-    def field_row(f, x):
+    def rim_tile(f, z, side):
+        at = 0 if side == 0 else rx - 8
         if f == 0:
-            return U.at[:, 8 + x, :]
+            return U.at[z, 8 + at:16 + at, :]
         if f == 1:
-            return V.at[:, x, :]
-        return PA.at[:, 8 + x, :]
+            return V.at[z, at:at + 8, :]
+        return PA.at[z, 8 + at:16 + at, :]
+
+    def keep_rim(side):
+        def part(i, _):
+            for k in range(10):
+                for f in range(3):
+                    FO[f, i * 10 + k] = rim_tile(f, i * 10 + k, side)[...]
+            return 0
+
+        lax.fori_loop(0, nz // 10, part, 0)
 
     def blend_x(side):
         me = 0 if side == 0 else ngx - 1
@@ -137,13 +169,25 @@
                 if n >= 3 * BAND:
                     continue
                 f, d = n // BAND, n % BAND
-                x = d if side == 0 else rx - 1 - d
-                rate = RW[x:x + 1, :].astype(F32)
-                weight = jnp.maximum(rate - float(d), 0.0) / rate
-                slab = turned[64 * half:64 * half + nz]
-                row = field_row(f, x)
-                old = row[...]
-                row[...] = old + weight * (slab - old)
+                QX[f, :, d if side == 0 else 7 - d, :] = turned[64 * half:64 * half + 64]
+        at = 0 if side == 0 else rx - 8
+        row = lax.broadcasted_iota(jnp.int32, (8, ly), 0).astype(F32)
+        dist = row if side == 0 else 7.0 - row
+        lane = lax.broadcasted_iota(jnp.int32, (8, ly), 1).astype(F32)
+        rate = RW[at:at + 8].astype(F32)
+        weight = jnp.maximum(rate - dist, 0.0) / rate
+        south = jnp.where(has_s, 0.0, jnp.maximum(rate - lane, 0.0) / rate)
+        north = jnp.where(has_n, 0.0, jnp.maximum(rate - ((ly - 1.0) - lane), 0.0) / rate)
+        weight = weight * ((1.0 - south) * (1.0 - north))
+
+        def part(i, _):
+            for k in range(10):
+                for f in range(3):
+                    tile = rim_tile(f, i * 10 + k, side)
+                    tile[...] = tile[...] + weight * (QX[f, i * 10 + k] - FO[f, i * 10 + k])
+            return 0
+
+        lax.fori_loop(0, nz // 10, part, 0)
 
     def blend_y(side):
         me = 0 if side == 0 else ngy - 1
@@ -152,23 +196,11 @@
                 SNB[k] = SPK[side]
             else:
                 sn_copy(side, k).wait_recv()
-        BB[...] = jnp.zeros_like(BB)
-        TT[...] = jnp.zeros_like(TT)
-        for i in range(8):
-            for k in range(ngy):
-                TT[k * sx:(k + 1) * sx, :] = SNB[k, i]
-            turned = jnp.transpose(TT[...])
-            for half in range(2):
-                n = i + 8 * half
-                if n >= 3 * BAND:
-                    continue
-                f, d = n // BAND, n % BAND
-                dd = d if side == 0 else 7 - d
-                BB[f, :, dd, :] = turned[64 * half:64 * half + 64]
-        for f in range(3):
+        for k in range(ngy):
             for q in range(4):
-                block = BB[f, 16 * q:16 * q + 16].reshape(128, 128)
-                QQ[f, q] = jnp.transpose(block)[:rx]
+                for f in range(3):
+                    at = (q * 3 + f) * sx
+                    QQ[f, q, k * sx:(k + 1) * sx, :] = SNB[k, at:at + sx, :]
         lane = lax.broadcasted_iota(jnp.int32, (rows, ly), 1).astype(F32)
         dist = lane if side == 0 else (ly - 1.0) - lane
 
@@ -192,10 +224,11 @@
 
         lax.fori_loop(0, GROUPS, part, 0)
 
+    QX[...] = jnp.zeros_like(QX)
     for side in range(2):
         @pl.when(gx == (0 if side == 0 else ngx - 1))
         def _(side=side):
-            blend_x(side)
+            keep_rim(side)
     for side in range(2):
         @pl.when(gy == (0 if side == 0 else ngy - 1))
         def _(side=side):
@@ -204,6 +237,7 @@
     pair = lax.broadcasted_iota(jnp.int32, (rows, ly), 1) // 2
     lane_r = lax.broadcasted_iota(jnp.int32, (rows, ly), 1)
     rim = (lane_r == 0) | (lane_r == ly - 1)
+    even = lax.rem(lane_r, 2) == 0
 
     def put(acc, value, z):
         return jnp.where(pair == z, pltpu.roll(value, (2 * z + 1) % 128, 1), acc)
@@ -215,7 +249,13 @@
         return pl.ds(pl.multiple_of(g * rows, 8), rows)
 
     def in_order(i):
-        return jnp.where(i == 0, 0, jnp.where(i == 1, GROUPS - 1, i - 1))
+        late = jnp.where(i == GROUPS - 1, 0, jnp.where(i == 0, GROUPS - 1, i))
+        both = jnp.where(i == 0, 0, jnp.where(i == 1, GROUPS - 1, i - 1))
+        return jnp.where(gx == 0, late, jnp.where(gx == ngx - 1, i, both))
+
+    def put_edges(par, g, acc):
+        EB[par, all_rows(g)] = acc
+        ES[par, all_rows(g)] = jnp.where(even, pltpu.roll(acc, 127, 1), pltpu.roll(acc, 1, 1))
 
     def x_west(par):
         return pltpu.make_async_remote_copy(
@@ -237,24 +277,21 @@
 
     def y_north(par, g):
         return pltpu.make_async_remote_copy(
-            src_ref=EB.at[par, all_rows(g)], dst_ref=RS.at[par, all_rows(g)],
+            src_ref=ES.at[par, all_rows(g)], dst_ref=RS.at[par, all_rows(g)],
             send_sem=ssem.at[2 + g, par], recv_sem=rsem.at[2 + g, par],
             device_id=(gx, gy + 1), device_id_type=MESH)
 
     def y_south(par, g):
         return pltpu.make_async_remote_copy(
-            src_ref=EB.at[par, all_rows(g)], dst_ref=RN.at[par, all_rows(g)],
+            src_ref=ES.at[par, all_rows(g)], dst_ref=RN.at[par, all_rows(g)],
             send_sem=ssem.at[6 + g, par], recv_sem=rsem.at[6 + g, par],
             device_id=(gx, gy - 1), device_id_type=MESH)
 
-    def v_north():
-        return pltpu.make_async_remote_copy(
-            src_ref=EV, dst_ref=RV,
-            send_sem=ssem.at[11, 0], recv_sem=rsem.at[11, 0],
+    def v_north(g):
+        return pltpu.make_async_remote_copy(
+            src_ref=EV.at[all_rows(g)], dst_ref=RV.at[all_rows(g)],
+            send_sem=ssem.at[11 + g, 0], recv_sem=rsem.at[11 + g, 0],
             device_id=(gx, gy + 1), device_id_type=MESH)
-
-    has_w, has_e = gx > 0, gx < ngx - 1
-    has_s, has_n = gy > 0, gy < ngy - 1
 
     def send_group(par, g):
         @pl.when((g == 0) & has_w)
@@ -263,7 +300,12 @@
 
         @pl.when((g == 0) & jnp.logical_not(has_w))
         def _():
-            P[par][:, 7, :] = P[par][:, 8, :]
+            def part(i, _):
+                for k in range(10):
+                    P[par][i * 10 + k, 7:8, :] = P[par][i * 10 + k, 8:9, :]
+                return 0
+
+            lax.fori_loop(0, nz // 10, part, 0)
 
         @pl.when((g == GROUPS - 1) & has_e)
         def _():
@@ -290,7 +332,13 @@
 
         @pl.when(g == GROUPS - 1)
         def _():
-            S[:, rx, :] = S[:, rx, :] + P[par][:, 8 + rx, :]
+            def part(i, _):
+                for k in range(10):
+                    z = i * 10 + k
+                    S[z, rx:rx + 1, :] = S[z, rx:rx + 1, :] + P[par][z, 8 + rx:9 + rx, :]
+                return 0
+
+            lax.fori_loop(0, nz // 10, part, 0)
 
         @pl.when(has_n)
         def _():
@@ -319,50 +367,44 @@
     def _():
         RV[...] = jnp.zeros_like(RV)
 
-    @pl.when(has_e)
-    def _():
-        u_east().start()
-
     def first(i, _):
         g = in_order(i)
-        acc_p = jnp.zeros((rows, ly), F32)
-        acc_v = jnp.zeros((rows, ly), F32)
+        acc = jnp.zeros((rows, ly), F32)
         for z in range(nz):
-            acc_p = put(acc_p, PA[z, own_rows(g)], z)
-            acc_v = put(acc_v, V[z, all_rows(g)], z)
-        EB[0, all_rows(g)] = acc_p
-        EV[all_rows(g)] = acc_v
+            acc = put(acc, PA[z, own_rows(g)], z)
+        put_edges(0, g, acc)
         send_group(0, g)
         return 0
 
-    lax.fori_loop(0, GROUPS, first, 0)
-
-    @pl.when(has_n)
-    def _():
-        v_north().start()
-
-    @pl.when(has_e)
-    def _():
-        u_east().wait_send()
-
-    @pl.when(has_w)
-    def _():
-        u_east().wait_recv()
-
-    @pl.when(has_n)
-    def _():
-        v_north().wait_send()
-
-    @pl.when(has_s)
-    def _():
-        v_north().wait_recv()
+    def first_v(i, _):
+        g = in_order(i)
+        acc = jnp.zeros((rows, ly), F32)
+        for z in range(nz):
+            acc = put(acc, V[z, all_rows(g)], z)
+        EV[all_rows(g)] = acc
+
+        @pl.when(has_n)
+        def _():
+            v_north(g).start()
+
+        return 0
 
     SN[...] = jnp.zeros_like(SN)
     S[:, rx, :] = jnp.zeros((nz, ly), F32)
     first_lane = lane_r == 0
     last_lane = lane_r == ly - 1
 
-    def divergence(g, _):
+    def divergence(i, _):
+        g = in_order(i)
+
+        @pl.when(has_n)
+        def _():
+            v_north(g).wait_send()
+
+        @pl.when(has_s)
+        def _():
+            v_north(g).wait_recv()
+
         halo_v = RV[all_rows(g)]
         for z in range(nz):
             u = U[z, own_rows(g)]
@@ -374,19 +416,36 @@
             S[z, all_rows(g)] = jnp.zeros((rows, ly), F32)
         return 0
 
-    lax.fori_loop(0, GROUPS, divergence, 0)
+    @pl.when(has_e)
+    def _():
+        u_east().start()
+
+    lax.fori_loop(0, GROUPS - 1, first, 0)
+    lax.fori_loop(0, GROUPS - 1, first_v, 0)
+
+    @pl.when(has_e)
+    def _():
+        u_east().wait_send()
+
+    @pl.when(has_w)
+    def _():
+        u_east().wait_recv()
+
+    lax.fori_loop(0, GROUPS - 1, divergence, 0)
+    for side in range(2):
+        @pl.when(gx == (0 if side == 0 else ngx - 1))
+        def _(side=side):
+            blend_x(side)
+    for part_of in (first, first_v, divergence):
+        lax.fori_loop(GROUPS - 1, GROUPS, part_of, 0)
 
     l_w.wait()
 
-    even = lax.rem(lane_r, 2) == 0
-
     def corrections(cur, g):
-        eb = EB[cur, all_rows(g)]
         rn = RN[cur, all_rows(g)]
-        rs = jnp.where(has_s, RS[cur, all_rows(g)], pltpu.roll(eb, 127, 1))
-        x = jnp.where(even, rs, rn) - eb
+        rs = jnp.where(has_s, RS[cur, all_rows(g)], EB[cur, all_rows(g)])
         SN[all_rows(g)] = SN[all_rows(g)] + rn
-        return jnp.where(even, pltpu.roll(x, 127, 1), pltpu.roll(x, 1, 1))
+        return jnp.where(even, rn, rs) - ES[cur, all_rows(g)]
 
     def forward(cur, nxt, g):
         rinv = 1.0 / R[all_rows(g)]
@@ -430,7 +489,7 @@
             if edges:
                 acc = put(acc, p, z + 1)
         if edges:
-            EB[nxt, all_rows(g)] = acc
+            put_edges(nxt, g, acc)
 
     def step(cur, nxt):
         def part(i, _):
@@ -451,37 +510,14 @@
     lax.fori_loop(0, (STEPS - 2) // 2, two_steps, 0)
     step(0, 1)
 
-    def stores(g, which):
-        to = lambda ref: ref.at[:, all_rows(g), :]
-        pairs = ((W.at[:, all_rows(g), :], to(wo_hbm)), (PA.at[:, own_rows(g), :], to(po_hbm)),
-                 (U.at[:, own_rows(g), :], to(uo_hbm)), (V.at[:, all_rows(g), :], to(vo_hbm)))
-        return [pltpu.make_async_copy(*pairs[k], osem.at[k, g]) for k in which]
-
     def last(i, _):
         g = in_order(i)
         wait_group(1, g)
         forward(1, 0, g)
         backward(0, g, False)
-        for c in stores(g, (0, 1)):
-            c.start()
         return 0
 
     lax.fori_loop(0, GROUPS, last, 0)
-
-    def winds(g, _):
-        halo = SN[all_rows(g)]
-        for z in range(nz):
-            t = S[z, all_rows(g)]
-            te = S[z, pl.ds(g * rows + 1, rows)]
-            tn = jnp.where(last_lane, pltpu.roll(halo, (254 - 2 * z) % 128, 1),
-                           pltpu.roll(t, 127, 1))
-            U[z, own_rows(g)] = U[z, own_rows(g)] - 0.3 * (te - t)
-            V[z, all_rows(g)] = V[z, all_rows(g)] - 0.3 * (tn - t)
-        for c in stores(g, (2, 3)):
-            c.start()
-        return 0
-
-    lax.fori_loop(0, GROUPS, winds, 0)
 
     for side in range(2):
         @pl.when(gx != (0 if side == 0 else ngx - 1))
@@ -491,9 +527,41 @@
         @pl.when(gy != (0 if side == 0 else ngy - 1))
         def _(side=side):
             sn_copy(side, gy).wait_send()
+
+
+def finish(nz, rx, ly, W, PA, U, V, S, SN, uo_hbm, vo_hbm, wo_hbm, po_hbm, UO, VO, osem):
+    rows = rx // GROUPS
+    store_w = pltpu.make_async_copy(W, wo_hbm, osem.at[0, GROUPS])
+    store_p = pltpu.make_async_copy(PA.at[:, pl.ds(8, rx), :], po_hbm, osem.at[1, GROUPS])
+    store_w.start()
+    store_p.start()
+    last_lane = lax.broadcasted_iota(jnp.int32, (rows, ly), 1) == ly - 1
+
+    def store(k, g):
+        src, dst = ((UO, uo_hbm), (VO, vo_hbm))[k]
+        at = pl.ds(pl.multiple_of(g * rows, 8), rows)
+        return pltpu.make_async_copy(src.at[:, at, :], dst.at[:, at, :], osem.at[k, g])
+
+    def winds(g, _):
+        at = pl.ds(pl.multiple_of(g * rows, 8), rows)
+        halo = SN[at]
+        for z in range(nz):
+            t = S[z, at]
+            te = S[z, pl.ds(g * rows + 1, rows)]
+            tn = jnp.where(last_lane, pltpu.roll(halo, (255 - 2 * z) % 128, 1),
+                           pltpu.roll(t, 127, 1))
+            UO[z, at] = U[z, pl.ds(pl.multiple_of(g * rows + 8, 8), rows)] - 0.3 * (te - t)
+            VO[z, at] = V[z, at] - 0.3 * (tn - t)
+        store(0, g).start()
+        store(1, g).start()
+        return 0
+
+    lax.fori_loop(0, GROUPS, winds, 0)
+    store_w.wait()
+    store_p.wait()
     for g in range(GROUPS):
-        for c in stores(g, range(4)):
-            c.wait()
+        store(0, g).wait()
+        store(1, g).wait()
 
 
 def per_device(ngx, ngy, u, v, w, p, r, we, sn, rate):
@@ -502,28 +570,40 @@
     sn = jnp.transpose(sn, (0, 1, 3, 4, 2))
     field = jax.ShapeDtypeStruct((nz, rx, ly), F32)
     vm = lambda *s: pltpu.VMEM(s, F32)
-    any_ = pl.BlockSpec(memory_space=pl.ANY)
+    hbm = pl.BlockSpec(memory_space=pltpu.HBM)
+    vmem = pl.BlockSpec(memory_space=pltpu.VMEM)
     dma = pltpu.SemaphoreType.DMA
+    sx = rx // ngy
     scratch = [
-        vm(nz, rx + 16, ly), vm(nz, rx + 16, ly), vm(nz, rx, ly), vm(nz, rx + 8, ly), vm(nz, rx, ly), vm(nz, rx, ly),
-        vm(nz, rx + 8, ly), vm(nz, rx, ly), vm(rx, ly), pltpu.VMEM((rx, ly), jnp.int32),
-        vm(2, 3, BAND, ly // ngx, nz), vm(2, 3, BAND, rx // ngy, nz),
-        vm(2, 8, ly // ngx, 128), vm(2, 8, rx // ngy, 128),
-        vm(ngx, 8, ly // ngx, 128), vm(ngy, 8, rx // ngy, 128),
-        vm(128, 128), vm(3, 64, 8, 128), vm(3, 4, rx, 128),
-        vm(2, rx, ly), vm(2, rx, ly), vm(2, rx, ly), vm(rx, ly), vm(rx, ly), vm(rx, ly), vm(rx, ly),
-        dma((8,)), dma((4, GROUPS)), dma((12, 2)), dma((12, 2)),
+        vm(nz, rx + 16, ly), vm(nz, rx, ly), vm(nz, rx, ly),
+        vm(rx, ly), pltpu.VMEM((rx, ly), jnp.int32),
+        vm(2, 3, BAND, ly // ngx, nz), vm(2, 3, BAND, sx, nz),
+        vm(2, 8, ly // ngx, 128), vm(2, 12 * sx, 128),
+        vm(ngx, 8, ly // ngx, 128), vm(ngy, 12 * sx, 128),
+        vm(128, 128), vm(64, 8, 128), vm(64, 8, 128), vm(3, 4, rx, 128), vm(3, nz, 8, ly),
+        vm(3, 64, 8, ly),
+        vm(2, rx, ly), vm(2, rx, ly), vm(2, rx, ly), vm(2, rx, ly), vm(rx, ly), vm(rx, ly),
+        dma((8,)), dma((11 + GROUPS, 2)), dma((11 + GROUPS, 2)),
         dma((2,)), dma((ngx,)), dma((2,)), dma((ngy,)),
     ]
-    return pl.pallas_call(
+    state = pl.pallas_call(
         functools.partial(kernel, ngx, ngy, nz, rx, ly),
-        out_shape=(field,) * 4,
-        in_specs=[any_] * 8,
-        out_specs=(any_,) * 4,
+        out_shape=(vm(nz, rx, ly), vm(nz, rx + 16, ly), vm(nz, rx + 8, ly), vm(nz, rx, ly),
+                   vm(nz, rx + 8, ly), vm(rx, ly)),
+        in_specs=[hbm] * 8,
+        out_specs=(vmem,) * 6,
         scratch_shapes=scratch,
         compiler_params=pltpu.CompilerParams(collective_id=0, has_side_effects=True,
-                                             vmem_limit_bytes=63 * 1024 * 1024),
-    )(u, v, w, p, r, we, sn, rate)
+                                             vmem_limit_bytes=30 * 1024 * 1024),
+    )(*(pltpu.with_memory_space_constraint(x, pltpu.HBM) for x in (u, v, w, p, r, we, sn, rate)))
+    return pl.pallas_call(
+        functools.partial(finish, nz, rx, ly),
+        out_shape=(field,) * 4,
+        in_specs=[vmem] * 6,
+        out_specs=(hbm,) * 4,
+        scratch_shapes=[vm(nz, rx, ly), vm(nz, rx, ly), dma((2, GROUPS + 1))],
+        compiler_params=pltpu.CompilerParams(vmem_limit_bytes=16 * 1024 * 1024),
+    )(*state)
 
 
 def solution(mesh):

time: 60.1 us -> 53.6 us (0.89); the launches traced: 59.9 us -> 52.6 us
  local copies, waits for them, and re-layouts: 8.97 us -> 0 us
  Pallas kernels: 50.3 us -> 52 us
    unnamed x10 -> x0, local copies, waits for them, and re-layouts: 8.97 us -> none
    pallas_call x0 -> x1, Pallas kernels: none -> 3.21 us  [per_device(): pl.pallas_call(functools.partial(finish, nz, rx, ly), out_shape=(field,)...]
    pallas_call x1, Pallas kernels: 50.3 us -> 48.8 us  [per_device(): pl.pallas_call(functools.partial(kernel, ngx, ngy, nz, rx, ly), out_shape...]
where the time goes in v3:
time: 53.6 us; the launch traced here: 52.6 us
  Pallas kernels  52 us (97%)
  between operations  0.64 us (1%)
    pallas_call x1, Pallas kernels, per_device(): pl.pallas_call(functools.partial(kernel, ngx, ngy, nz, rx, ly), out_shape...  48.8 us
    pallas_call x1, Pallas kernels, per_device(): pl.pallas_call(functools.partial(finish, nz, rx, ly), out_shape=(field,)...  3.21 us

profile of v3, /device:TPU:32, one launch (start us, length us, event | category | flops | bytes accessed | tf_op | source)
XLA Modules:
  0.0 52.6 jit_solution(792459309283362364)
XLA Ops:
  0.6 48.8 %shard_map.111 = (f32[60,64,128]{2,1,0:T(8,128)S(1)}, f32[60,80,128]{2,1,0:T(8,128)S(1)}, f32[60,72,128]{2,1,0:T(8,128)S(1)}, f32[60,64,128]{2,1,0:T(8,128)S(1)}...) custom-call(f32[60,64,128]{2,1,0:T(8,128)} %u_hbm.1, f32[60,64,128]{2,1,0:T(8,128)} %v_hbm.1, f32[60,64,128]{2,1,0:T(8,128)} %w_hbm.1, ...), custom_call_target="tpu_custom_call" | custom-call | tf_op jit(solution)/shard_map/pallas_call | solution.py:589
  49.4 3.2 %shard_map.112 = (f32[60,64,128]{2,1,0:T(8,128)}, f32[60,64,128]{2,1,0:T(8,128)}, f32[60,64,128]{2,1,0:T(8,128)}, f32[60,64,128]{2,1,0:T(8,128)}) custom-call(f32[60,64,128]{2,1,0:T(8,128)S(1)} %get-tuple-element.10.W, f32[60,80,128]{2,1,0:T(8,128)S(1)} %get-tuple-element.11.PA, f32[60,72,128]{2,1,0:T(8,128)S(1)} %get-tuple-element.12.U, ...), custom_call_target="tpu_custom_call" | custom-call | tf_op jit(solution)/shard_map/pallas_call | solution.py:599

commit v4 on v3

--- a/solution.py
+++ b/solution.py
@@ -95,7 +95,9 @@
     for q in range(4):
         for side, ref in enumerate((BB, BN)):
             block = jnp.transpose(ref[16 * q:16 * q + 16].reshape(128, 128))
-            SPK[side, q * 3 * sx:(q + 1) * 3 * sx, :] = block[side * 3 * sx:(side + 1) * 3 * sx]
+            for f in range(3):
+                at = (f * 4 + q) * sx
+                SPK[side, at:at + sx, :] = block[(side * 3 + f) * sx:(side * 3 + f + 1) * sx]
 
     l_r.wait()
     r_all = R[...]
@@ -116,20 +118,26 @@
             src_ref=WPK.at[side], dst_ref=WEB.at[k], send_sem=wssem.at[side],
             recv_sem=wrsem.at[k], device_id=(dest, gy), device_id_type=MESH)
 
-    def sn_copy(side, k):
+    def sn_rows(part):
+        return pl.ds(0, 8 * sx) if part else pl.ds(8 * sx, 4 * sx)
+
+    def sn_copy(side, k, part):
         dest = 0 if side == 0 else ngy - 1
         return pltpu.make_async_remote_copy(
-            src_ref=SPK.at[side], dst_ref=SNB.at[k], send_sem=sssem.at[side],
-            recv_sem=srsem.at[k], device_id=(gx, dest), device_id_type=MESH)
-
+            src_ref=SPK.at[side, sn_rows(part)], dst_ref=SNB.at[k, sn_rows(part)],
+            send_sem=sssem.at[side, part], recv_sem=srsem.at[k, part],
+            device_id=(gx, dest), device_id_type=MESH)
+
+    for act in ("start", "wait_send"):
+        for part in range(2):
+            for side in range(2):
+                @pl.when(gy != (0 if side == 0 else ngy - 1))
+                def _(side=side):
+                    getattr(sn_copy(side, gy, part), act)()
     for side in range(2):
         @pl.when(gx != (0 if side == 0 else ngx - 1))
         def _(side=side):
             we_copy(side, gx).start()
-
-        @pl.when(gy != (0 if side == 0 else ngy - 1))
-        def _(side=side):
-            sn_copy(side, gy).start()
 
     l_rate.wait()
     l_p.wait()
@@ -189,18 +197,20 @@
 
         lax.fori_loop(0, nz // 10, part, 0)
 
-    def blend_y(side):
+    def gather_y(side, part):
         me = 0 if side == 0 else ngy - 1
         for k in range(ngy):
             if k == me:
-                SNB[k] = SPK[side]
+                SNB[k, sn_rows(part)] = SPK[side, sn_rows(part)]
             else:
-                sn_copy(side, k).wait_recv()
+                sn_copy(side, k, part).wait_recv()
         for k in range(ngy):
-            for q in range(4):
-                for f in range(3):
-                    at = (q * 3 + f) * sx
+            for f in ((0, 1) if part else (2,)):
+                for q in range(4):
+                    at = (f * 4 + q) * sx
                     QQ[f, q, k * sx:(k + 1) * sx, :] = SNB[k, at:at + sx, :]
+
+    def blend_fields(side, fields):
         lane = lax.broadcasted_iota(jnp.int32, (rows, ly), 1).astype(F32)
         dist = lane if side == 0 else (ly - 1.0) - lane
 
@@ -208,7 +218,7 @@
             at = pl.multiple_of(g * rows, 8)
             rate = RW[pl.ds(at, rows)].astype(F32)
             weight = jnp.maximum(rate - dist, 0.0) / rate
-            for f in range(3):
+            for f in fields:
                 for z in range(nz):
                     shift = ((0 if side == 0 else 120) + 128 - 8 * (z % 16)) % 128
                     slab = pltpu.roll(QQ[f, z // 16, pl.ds(at, rows)], shift, 1)
@@ -232,7 +242,8 @@
     for side in range(2):
         @pl.when(gy == (0 if side == 0 else ngy - 1))
         def _(side=side):
-            blend_y(side)
+            gather_y(side, 0)
+            blend_fields(side, (2,))
 
     pair = lax.broadcasted_iota(jnp.int32, (rows, ly), 1) // 2
     lane_r = lax.broadcasted_iota(jnp.int32, (rows, ly), 1)
@@ -293,10 +304,23 @@
             send_sem=ssem.at[11 + g, 0], recv_sem=rsem.at[11 + g, 0],
             device_id=(gx, gy + 1), device_id_type=MESH)
 
-    def send_group(par, g):
+    def send_x(par, g):
         @pl.when((g == 0) & has_w)
         def _():
             x_west(par).start()
+
+        @pl.when((g == GROUPS - 1) & has_e)
+        def _():
+            x_east(par).start()
+
+    def send_y(par, g):
+        @pl.when(has_n)
+        def _():
+            y_north(par, g).start()
+
+        @pl.when(has_s)
+        def _():
+            y_south(par, g).start()
 
         @pl.when((g == 0) & jnp.logical_not(has_w))
         def _():
@@ -307,18 +331,6 @@
 
             lax.fori_loop(0, nz // 10, part, 0)
 
-        @pl.when((g == GROUPS - 1) & has_e)
-        def _():
-            x_east(par).start()
-
-        @pl.when(has_n)
-        def _():
-            y_north(par, g).start()
-
-        @pl.when(has_s)
-        def _():
-            y_south(par, g).start()
-
     def wait_group(par, g):
         @pl.when((g == 0) & has_w)
         def _():
@@ -330,16 +342,6 @@
             x_west(par).wait_recv()
             x_east(par).wait_send()
 
-        @pl.when(g == GROUPS - 1)
-        def _():
-            def part(i, _):
-                for k in range(10):
-                    z = i * 10 + k
-                    S[z, rx:rx + 1, :] = S[z, rx:rx + 1, :] + P[par][z, 8 + rx:9 + rx, :]
-                return 0
-
-            lax.fori_loop(0, nz // 10, part, 0)
-
         @pl.when(has_n)
         def _():
             y_south(par, g).wait_recv()
@@ -349,6 +351,12 @@
         def _():
             y_north(par, g).wait_recv()
             y_south(par, g).wait_send()
+
+    def s_west():
+        return pltpu.make_async_remote_copy(
+            src_ref=S.at[:, pl.ds(0, 1), :], dst_ref=S.at[:, pl.ds(rx, 1), :],
+            send_sem=ssem.at[10, 1], recv_sem=rsem.at[10, 1],
+            device_id=(gx - 1, gy), device_id_type=MESH)
 
     @pl.when(jnp.logical_not(has_w))
     def _():
@@ -372,8 +380,9 @@
         acc = jnp.zeros((rows, ly), F32)
         for z in range(nz):
             acc = put(acc, PA[z, own_rows(g)], z)
+        send_x(0, g)
         put_edges(0, g, acc)
-        send_group(0, g)
+        send_y(0, g)
         return 0
 
     def first_v(i, _):
@@ -390,7 +399,11 @@
         return 0
 
     SN[...] = jnp.zeros_like(SN)
-    S[:, rx, :] = jnp.zeros((nz, ly), F32)
+
+    @pl.when(jnp.logical_not(has_e))
+    def _():
+        S[:, rx, :] = jnp.zeros((nz, ly), F32)
+
     first_lane = lane_r == 0
     last_lane = lane_r == ly - 1
 
@@ -416,11 +429,17 @@
             S[z, all_rows(g)] = jnp.zeros((rows, ly), F32)
         return 0
 
+    lax.fori_loop(0, GROUPS - 1, first, 0)
+    for side in range(2):
+        @pl.when(gy == (0 if side == 0 else ngy - 1))
+        def _(side=side):
+            gather_y(side, 1)
+            blend_fields(side, (0, 1))
+
     @pl.when(has_e)
     def _():
         u_east().start()
 
-    lax.fori_loop(0, GROUPS - 1, first, 0)
     lax.fori_loop(0, GROUPS - 1, first_v, 0)
 
     @pl.when(has_e)
@@ -489,15 +508,20 @@
             if edges:
                 acc = put(acc, p, z + 1)
         if edges:
+            send_x(nxt, g)
             put_edges(nxt, g, acc)
 
-    def step(cur, nxt):
+    def step(cur, nxt, share=False):
         def part(i, _):
             g = in_order(i)
             wait_group(cur, g)
             forward(cur, nxt, g)
             backward(nxt, g, True)
-            send_group(nxt, g)
+            send_y(nxt, g)
+            if share:
+                @pl.when((g == 0) & has_w)
+                def _():
+                    s_west().start()
             return 0
 
         lax.fori_loop(0, GROUPS, part, 0)
@@ -508,25 +532,38 @@
         return 0
 
     lax.fori_loop(0, (STEPS - 2) // 2, two_steps, 0)
-    step(0, 1)
+    step(0, 1, share=True)
 
     def last(i, _):
         g = in_order(i)
         wait_group(1, g)
+
+        @pl.when((g == 0) & has_w)
+        def _():
+            s_west().wait_send()
+
         forward(1, 0, g)
         backward(0, g, False)
         return 0
 
     lax.fori_loop(0, GROUPS, last, 0)
+
+    @pl.when(has_e)
+    def _():
+        s_west().wait_recv()
+
+        def part(i, _):
+            for k in range(10):
+                z = i * 10 + k
+                S[z, rx:rx + 1, :] = S[z, rx:rx + 1, :] + PB[z, 8 + rx:9 + rx, :]
+            return 0
+
+        lax.fori_loop(0, nz // 10, part, 0)
 
     for side in range(2):
         @pl.when(gx != (0 if side == 0 else ngx - 1))
         def _(side=side):
             we_copy(side, gx).wait_send()
-
-        @pl.when(gy != (0 if side == 0 else ngy - 1))
-        def _(side=side):
-            sn_copy(side, gy).wait_send()
 
 
 def finish(nz, rx, ly, W, PA, U, V, S, SN, uo_hbm, vo_hbm, wo_hbm, po_hbm, UO, VO, osem):
@@ -584,7 +621,7 @@
         vm(3, 64, 8, ly),
         vm(2, rx, ly), vm(2, rx, ly), vm(2, rx, ly), vm(2, rx, ly), vm(rx, ly), vm(rx, ly),
         dma((8,)), dma((11 + GROUPS, 2)), dma((11 + GROUPS, 2)),
-        dma((2,)), dma((ngx,)), dma((2,)), dma((ngy,)),
+        dma((2,)), dma((ngx,)), dma((2, 2)), dma((ngy, 2)),
     ]
     state = pl.pallas_call(
         functools.partial(kernel, ngx, ngy, nz, rx, ly),

time: 53.6 us -> 51.2 us (0.955)
  Pallas kernels: 52 us -> 49.9 us
    pallas_call x1, Pallas kernels: 48.8 us -> 46.7 us  [per_device(): pl.pallas_call(functools.partial(kernel, ngx, ngy, nz, rx, ly), out_shape...]
where the time goes in v4:
time: 51.2 us; the launch traced here: 50.5 us
  Pallas kernels  49.9 us (97%)
  between operations  0.64 us (1%)
    pallas_call x1, Pallas kernels, per_device(): pl.pallas_call(functools.partial(kernel, ngx, ngy, nz, rx, ly), out_shape...  46.7 us
    pallas_call x1, Pallas kernels, per_device(): pl.pallas_call(functools.partial(finish, nz, rx, ly), out_shape=(field,)...  3.21 us

profile of v4, /device:TPU:32, one launch (start us, length us, event | category | flops | bytes accessed | tf_op | source)
XLA Modules:
  0.0 50.5 jit_solution(3339270223678951367)
XLA Ops:
  0.6 46.7 %shard_map.111 = (f32[60,64,128]{2,1,0:T(8,128)S(1)}, f32[60,80,128]{2,1,0:T(8,128)S(1)}, f32[60,72,128]{2,1,0:T(8,128)S(1)}, f32[60,64,128]{2,1,0:T(8,128)S(1)}...) custom-call(f32[60,64,128]{2,1,0:T(8,128)} %u_hbm.1, f32[60,64,128]{2,1,0:T(8,128)} %v_hbm.1, f32[60,64,128]{2,1,0:T(8,128)} %w_hbm.1, ...), custom_call_target="tpu_custom_call" | custom-call | tf_op jit(solution)/shard_map/pallas_call | solution.py:626
  47.3 3.2 %shard_map.112 = (f32[60,64,128]{2,1,0:T(8,128)}, f32[60,64,128]{2,1,0:T(8,128)}, f32[60,64,128]{2,1,0:T(8,128)}, f32[60,64,128]{2,1,0:T(8,128)}) custom-call(f32[60,64,128]{2,1,0:T(8,128)S(1)} %get-tuple-element.10.W, f32[60,80,128]{2,1,0:T(8,128)S(1)} %get-tuple-element.11.PA, f32[60,72,128]{2,1,0:T(8,128)S(1)} %get-tuple-element.12.U, ...), custom_call_target="tpu_custom_call" | custom-call | tf_op jit(solution)/shard_map/pallas_call | solution.py:636

commit v5 on v4

--- a/solution.py
+++ b/solution.py
@@ -210,7 +210,7 @@
                     at = (f * 4 + q) * sx
                     QQ[f, q, k * sx:(k + 1) * sx, :] = SNB[k, at:at + sx, :]
 
-    def blend_fields(side, fields):
+    def blend_fields(side, fields, group=None):
         lane = lax.broadcasted_iota(jnp.int32, (rows, ly), 1).astype(F32)
         dist = lane if side == 0 else (ly - 1.0) - lane
 
@@ -232,7 +232,10 @@
                     dst[...] = old + weight * (slab - old)
             return 0
 
-        lax.fori_loop(0, GROUPS, part, 0)
+        if group is None:
+            lax.fori_loop(0, GROUPS, part, 0)
+        else:
+            part(group, 0)
 
     QX[...] = jnp.zeros_like(QX)
     for side in range(2):
@@ -243,7 +246,6 @@
         @pl.when(gy == (0 if side == 0 else ngy - 1))
         def _(side=side):
             gather_y(side, 0)
-            blend_fields(side, (2,))
 
     pair = lax.broadcasted_iota(jnp.int32, (rows, ly), 1) // 2
     lane_r = lax.broadcasted_iota(jnp.int32, (rows, ly), 1)
@@ -377,10 +379,10 @@
 
     def first(i, _):
         g = in_order(i)
+        send_x(0, g)
         acc = jnp.zeros((rows, ly), F32)
         for z in range(nz):
             acc = put(acc, PA[z, own_rows(g)], z)
-        send_x(0, g)
         put_edges(0, g, acc)
         send_y(0, g)
         return 0
@@ -406,6 +408,20 @@
 
     first_lane = lane_r == 0
     last_lane = lane_r == ly - 1
+
+    def own_part(p):
+        return 0.09 * (4.0 * p - (pltpu.roll(p, 1, 1) + pltpu.roll(p, 127, 1)))
+
+    def ahead(par):
+        def part(i, _):
+            g = in_order(i)
+            for z in range(nz):
+                p = P[par][z, own_rows(g)]
+                E[z, all_rows(g)] = E[z, all_rows(g)] + own_part(p)
+                S[z, all_rows(g)] = S[z, all_rows(g)] + p
+            return 0
+
+        lax.fori_loop(0, GROUPS, part, 0)
 
     def divergence(i, _):
         g = in_order(i)
@@ -425,11 +441,30 @@
             v = V[z, all_rows(g)]
             vs = jnp.where(first_lane, pltpu.roll(halo_v, (128 - 2 * z) % 128, 1),
                            pltpu.roll(v, 1, 1))
-            E[z, all_rows(g)] = 0.3 * ((u - uw) + (v - vs))
-            S[z, all_rows(g)] = jnp.zeros((rows, ly), F32)
+            p = PA[z, own_rows(g)]
+            E[z, all_rows(g)] = 0.3 * ((u - uw) + (v - vs)) + own_part(p)
+            S[z, all_rows(g)] = p
         return 0
 
-    lax.fori_loop(0, GROUPS - 1, first, 0)
+    def blend_p(i):
+        for side in range(2):
+            @pl.when(gy == (0 if side == 0 else ngy - 1))
+            def _(side=side):
+                blend_fields(side, (2,), in_order(i))
+
+    def blend_first(i, _):
+        blend_p(i)
+        first(i, 0)
+        return 0
+
+    at_end = jnp.logical_not(has_w & has_e)
+    now = jnp.where(at_end, GROUPS - 1, GROUPS)
+    lax.fori_loop(0, now, blend_first, 0)
+
+    @pl.when(at_end)
+    def _():
+        blend_p(GROUPS - 1)
+
     for side in range(2):
         @pl.when(gy == (0 if side == 0 else ngy - 1))
         def _(side=side):
@@ -440,7 +475,7 @@
     def _():
         u_east().start()
 
-    lax.fori_loop(0, GROUPS - 1, first_v, 0)
+    lax.fori_loop(0, now, first_v, 0)
 
     @pl.when(has_e)
     def _():
@@ -450,13 +485,13 @@
     def _():
         u_east().wait_recv()
 
-    lax.fori_loop(0, GROUPS - 1, divergence, 0)
+    lax.fori_loop(0, now, divergence, 0)
     for side in range(2):
         @pl.when(gx == (0 if side == 0 else ngx - 1))
         def _(side=side):
             blend_x(side)
     for part_of in (first, first_v, divergence):
-        lax.fori_loop(GROUPS - 1, GROUPS, part_of, 0)
+        lax.fori_loop(now, GROUPS, part_of, 0)
 
     l_w.wait()
 
@@ -474,12 +509,9 @@
             p = P[cur][z, own_rows(g)]
             pe = P[cur][z, pl.ds(9 + g * rows, rows)]
             pw = P[cur][z, pl.ds(7 + g * rows, rows)]
-            ns = pltpu.roll(p, 1, 1) + pltpu.roll(p, 127, 1)
             k = jnp.where(rim, pltpu.roll(k_g, (255 - 2 * z) % 128, 1), 0.0)
-            total = (pe + pw) + (ns + k)
-            e = E[z, all_rows(g)] + 0.09 * (4.0 * p - total)
+            e = E[z, all_rows(g)] - 0.09 * ((pe + pw) + k)
             E[z, all_rows(g)] = e
-            S[z, all_rows(g)] = S[z, all_rows(g)] + p
             q = p - e
             P[nxt][z, own_rows(g)] = q
             return q
@@ -512,19 +544,26 @@
             put_edges(nxt, g, acc)
 
     def step(cur, nxt, share=False):
+        if share:
+            @pl.when(has_w)
+            def _():
+                s_west().start()
+
         def part(i, _):
             g = in_order(i)
             wait_group(cur, g)
             forward(cur, nxt, g)
             backward(nxt, g, True)
             send_y(nxt, g)
-            if share:
-                @pl.when((g == 0) & has_w)
-                def _():
-                    s_west().start()
             return 0
 
         lax.fori_loop(0, GROUPS, part, 0)
+        if share:
+            @pl.when(has_w)
+            def _():
+                s_west().wait_send()
+
+        ahead(nxt)
 
     def two_steps(i, _):
         step(0, 1)
@@ -534,14 +573,10 @@
     lax.fori_loop(0, (STEPS - 2) // 2, two_steps, 0)
     step(0, 1, share=True)
 
+
     def last(i, _):
         g = in_order(i)
         wait_group(1, g)
-
-        @pl.when((g == 0) & has_w)
-        def _():
-            s_west().wait_send()
-
         forward(1, 0, g)
         backward(0, g, False)
         return 0

time: 51.2 us -> 49.5 us (0.967); the launches traced: 50.5 us -> 49.4 us
  Pallas kernels: 49.9 us -> 48.7 us
    pallas_call x1, Pallas kernels: 46.7 us -> 45.5 us  [per_device(): pl.pallas_call(functools.partial(kernel, ngx, ngy, nz, rx, ly), out_shape...]
where the time goes in v5:
time: 49.5 us; the launch traced here: 49.4 us
  Pallas kernels  48.7 us (98%)
  between operations  0.64 us (1%)
    pallas_call x1, Pallas kernels, per_device(): pl.pallas_call(functools.partial(kernel, ngx, ngy, nz, rx, ly), out_shape...  45.5 us
    pallas_call x1, Pallas kernels, per_device(): pl.pallas_call(functools.partial(finish, nz, rx, ly), out_shape=(field,)...  3.21 us

profile of v5, /device:TPU:32, one launch (start us, length us, event | category | flops | bytes accessed | tf_op | source)
XLA Modules:
  0.0 49.4 jit_solution(9493983499526504947)
XLA Ops:
  0.6 45.5 %shard_map.111 = (f32[60,64,128]{2,1,0:T(8,128)S(1)}, f32[60,80,128]{2,1,0:T(8,128)S(1)}, f32[60,72,128]{2,1,0:T(8,128)S(1)}, f32[60,64,128]{2,1,0:T(8,128)S(1)}...) custom-call(f32[60,64,128]{2,1,0:T(8,128)} %u_hbm.1, f32[60,64,128]{2,1,0:T(8,128)} %v_hbm.1, f32[60,64,128]{2,1,0:T(8,128)} %w_hbm.1, ...), custom_call_target="tpu_custom_call" | custom-call | tf_op jit(solution)/shard_map/pallas_call | solution.py:661
  46.2 3.2 %shard_map.112 = (f32[60,64,128]{2,1,0:T(8,128)}, f32[60,64,128]{2,1,0:T(8,128)}, f32[60,64,128]{2,1,0:T(8,128)}, f32[60,64,128]{2,1,0:T(8,128)}) custom-call(f32[60,64,128]{2,1,0:T(8,128)S(1)} %get-tuple-element.10.W, f32[60,80,128]{2,1,0:T(8,128)S(1)} %get-tuple-element.11.PA, f32[60,72,128]{2,1,0:T(8,128)S(1)} %get-tuple-element.12.U, ...), custom_call_target="tpu_custom_call" | custom-call | tf_op jit(solution)/shard_map/pallas_call | solution.py:671
